TPU v7x, 32 devices: a whole 2x2x4 slice. The times are simulated.
32 devices in a mesh: layer: 2 (over x), lat: 16 (over z, y, core).
Axes of the slice: x: 2, y: 2, z: 4, core: 2. Of those that a mesh axis runs over, the one named last changes fastest.
Arguments:
- acts: bfloat16 [2, 256, 1280], P('layer', 'lat'), may hold values from -6 to 6
- enc_weight: bfloat16 [2, 1280, 8192], P('layer', None, 'lat'), may hold values from -0.15625 to 0.15625
- enc_bias: float32 [2, 8192], P('layer', 'lat'), may hold values from -3 to 3
- dec_weight: bfloat16 [2, 2, 8192, 1280], P('layer', None, 'lat'), may hold values from -0.0625 to 0.0625
- dec_bias: float32 [2, 1280], P('layer'), may hold values from -3 to 3
Outputs:
- recon: bfloat16 [2, 256, 1280], P('layer', 'lat')
All inputs are finite; a program needn't handle non-finite values.
Results may differ from a plain program's by a relative error of at most 0.0048.
Values may be sent and summed in bfloat16 or wider, within the bound.
No kernel may reach another device: no remote copies, remote signals or barrier semaphores. Data moves between devices by JAX's collectives and lax.ppermute only.
A program may use at most 128 MiB of HBM per device.

v0:
```python
import functools

import jax
import jax.numpy as jnp
from jax import lax
from jax.experimental import pallas as pl
from jax.experimental.pallas import tpu as pltpu
from jax.sharding import PartitionSpec as P


BF16 = jnp.bfloat16
F32 = jnp.float32
VMEM = pl.BlockSpec(memory_space=pltpu.VMEM)
HBM = pl.BlockSpec(memory_space=pltpu.HBM)
MIB = 1 << 20


def factors(n):
    core = min(2, n)
    outer = min(4, n // core)
    return outer, n // core // outer, core


def swap(x, n, k):
    return lax.ppermute(x, "lat", [(i, i ^ k) for i in range(n)])


def call(kernel, outs, args, specs=None, scratch=(), flops=1000000):
    return pl.pallas_call(
        kernel,
        out_shape=outs,
        in_specs=specs or [VMEM] * len(args),
        out_specs=[VMEM] * len(outs),
        scratch_shapes=list(scratch),
        compiler_params=pltpu.CompilerParams(vmem_limit_bytes=8 * MIB),
        cost_estimate=pl.CostEstimate(flops=flops, bytes_accessed=MIB, transcendentals=0),
    )(*args)


def load_kernel(count, *refs):
    sems = refs[2 * count]
    copies = [pltpu.make_async_copy(refs[i], refs[count + i], sems.at[i]) for i in range(count)]
    for copy in copies:
        copy.start()
    for copy in copies:
        copy.wait()


def load(*arrays):
    arrays = [pltpu.with_memory_space_constraint(a, pltpu.HBM) for a in arrays]
    count = len(arrays)
    return call(
        functools.partial(load_kernel, count),
        [jax.ShapeDtypeStruct(a.shape, a.dtype) for a in arrays],
        arrays,
        specs=[HBM] * count,
        scratch=[pltpu.SemaphoreType.DMA((count,))],
    )


def stack_kernel(*refs):
    out = refs[-1]
    at = 0
    for ref in refs[:-1]:
        out[pl.ds(at, ref.shape[0]), :] = ref[...]
        at += ref.shape[0]


def stack(pieces):
    rows = sum(p.shape[0] for p in pieces)
    shape = jax.ShapeDtypeStruct((rows, pieces[0].shape[1]), pieces[0].dtype)
    return call(stack_kernel, [shape], pieces)[0]


def encode(x, w_refs, b_refs, latent):
    for c, (w, b) in enumerate(zip(w_refs, b_refs)):
        size = w.shape[2]
        pre = jnp.dot(x[...], w[0], preferred_element_type=F32) + b[...]
        latent[:, c * size : (c + 1) * size] = jnp.maximum(pre, 0.0).astype(BF16)


def decode(latent, w_refs, d, layers, out):
    target = lax.axis_index("layer") + d

    @pl.when(target < layers)
    def _():
        total = None
        for c, w in enumerate(w_refs):
            size = w.shape[2]
            part = jnp.dot(latent[:, c * size : (c + 1) * size], w[0, target], preferred_element_type=F32)
            total = part if total is None else total + part
        out[...] = total.astype(out.dtype)

    if d:

        @pl.when(target >= layers)
        def _():
            out[...] = jnp.zeros_like(out)


def encode_kernel(core, ds, layers, x, *refs):
    w_refs, b_refs, d_refs = refs[:core], refs[core : 2 * core], refs[2 * core : 3 * core]
    latent, outs = refs[3 * core], refs[3 * core + 1 :]
    encode(x, w_refs, b_refs, latent)
    for d, out in zip(ds, outs):
        decode(latent, d_refs, d, layers, out)


def decode_kernel(core, layers, latent, *refs):
    decode(latent, refs[:core], 0, layers, refs[core])


def work(acts, enc_weight, enc_bias, dec_weight, dec_bias):
    layers = lax.axis_size("layer")
    n = lax.axis_size("lat")
    outer, middle, core = factors(n)
    width = acts.shape[2]
    size = enc_weight.shape[2]

    pieces = [swap(acts[0], n, k * middle * core) for k in range(1, outer)]
    enc = [swap(enc_weight, n, k) for k in range(1, core)]
    dec = [swap(dec_weight, n, k) for k in range(1, core)]
    bias = [swap(enc_bias, n, k) for k in range(1, core)]
    own, own_enc, own_bias, own_dec = load(acts[0], enc_weight, enc_bias, dec_weight)
    enc, dec, bias = [own_enc] + enc, [own_dec] + dec, [own_bias] + bias
    column = stack([own] + pieces)
    xs = [column] + [swap(column, n, k * core) for k in range(1, middle)]
    rows = column.shape[0]
    flops = 2 * rows * core * size * width
    hidden = jax.ShapeDtypeStruct((rows, core * size), BF16)

    def send(part, d, k):
        pairs = [
            (l * n + i, (l + d) % layers * n + (i ^ (k * core) if l + d < layers else i))
            for l in range(layers)
            for i in range(n)
        ]
        return lax.ppermute(part, ("layer", "lat"), pairs)

    received = []
    total = None
    later = list(range(layers - 1, 0, -1))
    for k, x in enumerate(xs):
        ds = later if k else later + [0]
        outs = [jax.ShapeDtypeStruct((rows, width), BF16 if d else F32) for d in ds]
        latent, *parts = call(
            functools.partial(encode_kernel, core, ds, layers),
            [hidden] + outs,
            [x] + enc + bias + dec,
            flops=flops * (1 + len(ds)),
        )
        for d, part in zip(ds, parts):
            if d:
                received.append(send(part, d, k))
            else:
                total = part
        if k:
            part = call(
                functools.partial(decode_kernel, core, layers),
                [jax.ShapeDtypeStruct((rows, width), BF16)],
                [latent] + dec,
                flops=flops,
            )[0]
            received.append(send(part, 0, k))
    for piece in received:
        total = total + piece.astype(F32)
    pieces = total.reshape(outer, -1, width)
    total = pieces[0]
    for k in range(1, outer):
        total = total + swap(pieces[k].astype(BF16), n, k * middle * core).astype(F32)
    return (total + dec_bias[0][None, :]).astype(BF16)[None]


def solution(mesh):
    return jax.shard_map(
        work,
        mesh=mesh,
        in_specs=(
            P("layer", "lat", None),
            P("layer", None, "lat"),
            P("layer", "lat"),
            P("layer", None, "lat", None),
            P("layer", None),
        ),
        out_specs=P("layer", "lat", None),
        check_vma=False,
    )
```

profile of v0, /device:TPU:0, one launch (start us, length us, event | category | flops | bytes accessed | tf_op | source)
XLA Modules:
  0.0 36.7 jit_solution(5663443582716723296)
XLA Ops:
  0.0 0.0 copy-start.1
  0.0 0.5 %collective-permute-start.5 = (bf16[1,2,512,1280]{3,2,1,0:T(8,128)(2,1)}, bf16[1,2,512,1280]{3,2,1,0:T(8,128)(2,1)S(1)}, u32[]{:S(2)}, u32[]{:S(2)}) collective-permute-start(bf16[1,2,512,1280]{3,2,1,0:T(8,128)(2,1)} %refs_3_.1), channel_id=1, source_target_pairs={{0,1},{1,0},{2,3},{3,2},{4,5},{5,4},{6,7},{7,6},{8,9},{9,8},{10,11... | collective-permute-start | bytes 7864328 | tf_op jit(solution)/shard_map/ppermute | solution.py:25
  0.5 0.1 collective-permute-start.3
  0.6 5.0 %collective-permute-start.2 = (bf16[16,1280]{1,0:T(8,128)(2,1)}, bf16[16,1280]{1,0:T(8,128)(2,1)S(1)}, u32[]{:S(2)}, u32[]{:S(2)}) collective-permute-start(bf16[16,1280]{1,0:T(8,128)(2,1)} %bitcast.3), channel_id=1, source_target_pairs={{0,12},{1,13},{2,14},{3,15},{4,8},{5,9},{6,10},{7,11},{8,4},{9,5},... | collective-permute-start | bytes 122888 | tf_op jit(solution)/shard_map/ppermute | solution.py:25
  5.6 0.0 collective-permute-start.1
  5.6 0.6 %collective-permute-start = (bf16[16,1280]{1,0:T(8,128)(2,1)}, bf16[16,1280]{1,0:T(8,128)(2,1)S(1)}, u32[]{:S(2)}, u32[]{:S(2)}) collective-permute-start(bf16[16,1280]{1,0:T(8,128)(2,1)} %bitcast.5), channel_id=1, source_target_pairs={{0,4},{1,5},{2,6},{3,7},{4,0},{5,1},{6,2},{7,3},{8,12},{9,13},{10,... | collective-permute-start | bytes 122888 | tf_op jit(solution)/shard_map/ppermute | solution.py:25
  6.2 2.2 %shard_map.55 = (bf16[16,1280]{1,0:T(8,128)(2,1)S(1)}, bf16[1,1280,512]{2,1,0:T(8,128)(2,1)S(1)}, f32[1,512]{1,0:T(1,128)S(1)}, bf16[1,2,512,1280]{3,2,1,0:T(8,128)(2,1)S(1)}) custom-call(bf16[16,1280]{1,0:T(8,128)(2,1)} %bitcast.6, bf16[1,1280,512]{2,1,0:T(8,128)(2,1)} %refs_1_.1, f32[1,512]{1,0:T(1,128)} %refs_2_.1, bf16[1,2,512,1280]{3,2,1,0:T(8,128)(2,1)} %refs_3_.1), custom_call_target="tpu_custom_call" | custom-call | flops 1000000 | bytes 1048576 | tf_op jit(solution)/shard_map/pallas_call | solution.py:29
  8.4 0.0 collective-permute-done.2.refs_3_
  8.4 2.3 %collective-permute-done.1.refs_2_ = bf16[16,1280]{1,0:T(8,128)(2,1)S(1)} collective-permute-done((bf16[16,1280]{1,0:T(8,128)(2,1)}, bf16[16,1280]{1,0:T(8,128)(2,1)S(1)}, u32[]{:S(2)}, u32[]{:S(2)}) %collective-permute-start.1) | collective-permute-done | bytes 40992 | tf_op jit(solution)/shard_map/ppermute | solution.py:25
  10.7 0.0 collective-permute-done.refs_1_
  10.7 1.6 %collective-permute-start.7 = (bf16[64,1280]{1,0:T(8,128)(2,1)S(1)}, bf16[64,1280]{1,0:T(8,128)(2,1)S(1)}, u32[]{:S(2)}, u32[]{:S(2)}) collective-permute-start(bf16[64,1280]{1,0:T(8,128)(2,1)S(1)} %shard_map.56.x), channel_id=1, source_target_pairs={{0,2},{1,3},{2,0},{3,1},{4,6},{5,7},{6,4},{7,5},{8,10},{9,11},{10,... | collective-permute-start | bytes 491528 | tf_op jit(solution)/shard_map/ppermute | solution.py:25
  12.3 0.0 copy-done.1
  12.3 0.0 collective-permute-start.4
  12.3 1.2 %collective-permute-done.4.refs_3_ = f32[1,512]{1,0:T(1,128)S(1)} collective-permute-done((f32[1,512]{1,0:T(1,128)S(1)}, f32[1,512]{1,0:T(1,128)S(1)}, u32[]{:S(2)}, u32[]{:S(2)}) %collective-permute-start.4) | collective-permute-done | bytes 2080 | tf_op jit(solution)/shard_map/ppermute | solution.py:25
  13.5 2.6 %collective-permute-done.7.x = bf16[64,1280]{1,0:T(8,128)(2,1)S(1)} collective-permute-done((bf16[64,1280]{1,0:T(8,128)(2,1)S(1)}, bf16[64,1280]{1,0:T(8,128)(2,1)S(1)}, u32[]{:S(2)}, u32[]{:S(2)}) %collective-permute-start.7) | collective-permute-done | bytes 163872 | tf_op jit(solution)/shard_map/ppermute | solution.py:25
  16.1 0.0 collective-permute-done.3.refs_1_
  16.1 0.0 collective-permute-done.5.refs_5_.refs_1_
  16.1 1.1 %shard_map.58 = (bf16[64,1024]{1,0:T(8,128)(2,1)S(1)}, bf16[64,1280]{1,0:T(8,128)(2,1)S(1)}) custom-call(bf16[64,1280]{1,0:T(8,128)(2,1)S(1)} %collective-permute-done.7.x, bf16[1,1280,512]{2,1,0:T(8,128)(2,1)S(1)} %get-tuple-element.14.refs_0_, bf16[1,1280,512]{2,1,0:T(8,128)(2,1)S(1)} %collective-permute-done.3.refs_1_, ...), custom_call_target="tpu_custom_call" | custom-call | flops 335544320 | bytes 1048576 | tf_op jit(solution)/shard_map/pallas_call | solution.py:29
  17.3 1.9 %collective-permute-start.8 = (bf16[64,1280]{1,0:T(8,128)(2,1)S(1)}, bf16[64,1280]{1,0:T(8,128)(2,1)S(1)}, u32[]{:S(2)}, u32[]{:S(2)}) collective-permute-start(bf16[64,1280]{1,0:T(8,128)(2,1)S(1)} %get-tuple-element.19), channel_id=1, source_target_pairs={{0,18},{1,19},{2,16},{3,17},{4,22},{5,23},{6,20},{7,21},{8,26},{9,... | collective-permute-start | bytes 491528 | tf_op jit(solution)/shard_map/ppermute | solution.py:138
  19.2 0.6 %shard_map.59 = bf16[64,1280]{1,0:T(8,128)(2,1)S(1)} custom-call(bf16[64,1024]{1,0:T(8,128)(2,1)S(1)} %get-tuple-element.20.latent, bf16[1,2,512,1280]{3,2,1,0:T(8,128)(2,1)S(1)} %get-tuple-element.16.refs_4_.refs_0_, bf16[1,2,512,1280]{3,2,1,0:T(8,128)(2,1)S(1)} %collective-permute-done.5.refs_5_.refs_1_), custom_call_target="tpu_custom_call" | custom-call | flops 167772160 | bytes 1048576 | tf_op jit(solution)/shard_map/pallas_call | solution.py:29
  19.8 0.0 copy-start
  19.8 0.6 %collective-permute-start.9 = (bf16[64,1280]{1,0:T(8,128)(2,1)S(1)}, bf16[64,1280]{1,0:T(8,128)(2,1)S(1)}, u32[]{:S(2)}, u32[]{:S(2)}) collective-permute-start(bf16[64,1280]{1,0:T(8,128)(2,1)S(1)} %shard_map.59), channel_id=1, source_target_pairs={{0,2},{1,3},{2,0},{3,1},{4,6},{5,7},{6,4},{7,5},{8,10},{9,11},{10,... | collective-permute-start | bytes 491528 | tf_op jit(solution)/shard_map/ppermute | solution.py:138
  20.4 1.8 %shard_map.57 = (bf16[64,1024]{1,0:T(8,128)(2,1)}, bf16[64,1280]{1,0:T(8,128)(2,1)S(1)}, f32[64,1280]{1,0:T(8,128)S(1)}) custom-call(bf16[64,1280]{1,0:T(8,128)(2,1)S(1)} %shard_map.56.x, bf16[1,1280,512]{2,1,0:T(8,128)(2,1)S(1)} %get-tuple-element.14.refs_0_, bf16[1,1280,512]{2,1,0:T(8,128)(2,1)S(1)} %collective-permute-done.3.refs_1_, ...), custom_call_target="tpu_custom_call" | custom-call | flops 503316480 | bytes 1048576 | tf_op jit(solution)/shard_map/pallas_call | solution.py:29
  22.2 0.6 %collective-permute-start.6 = (bf16[64,1280]{1,0:T(8,128)(2,1)S(1)}, bf16[64,1280]{1,0:T(8,128)(2,1)S(1)}, u32[]{:S(2)}, u32[]{:S(2)}) collective-permute-start(bf16[64,1280]{1,0:T(8,128)(2,1)S(1)} %get-tuple-element.18), channel_id=1, source_target_pairs={{0,16},{1,17},{2,18},{3,19},{4,20},{5,21},{6,22},{7,23},{8,24},{9,... | collective-permute-start | bytes 491528 | tf_op jit(solution)/shard_map/ppermute | solution.py:138
  22.8 1.0 %collective-permute-done.8 = bf16[64,1280]{1,0:T(8,128)(2,1)S(1)} collective-permute-done((bf16[64,1280]{1,0:T(8,128)(2,1)S(1)}, bf16[64,1280]{1,0:T(8,128)(2,1)S(1)}, u32[]{:S(2)}, u32[]{:S(2)}) %collective-permute-start.8) | collective-permute-done | bytes 163872 | tf_op jit(solution)/shard_map/ppermute | solution.py:138
  23.8 1.4 %collective-permute-done.9 = bf16[64,1280]{1,0:T(8,128)(2,1)S(1)} collective-permute-done((bf16[64,1280]{1,0:T(8,128)(2,1)S(1)}, bf16[64,1280]{1,0:T(8,128)(2,1)S(1)}, u32[]{:S(2)}, u32[]{:S(2)}) %collective-permute-start.9) | collective-permute-done | bytes 163872 | tf_op jit(solution)/shard_map/ppermute | solution.py:138
  25.2 2.3 %collective-permute-done.6 = bf16[64,1280]{1,0:T(8,128)(2,1)S(1)} collective-permute-done((bf16[64,1280]{1,0:T(8,128)(2,1)S(1)}, bf16[64,1280]{1,0:T(8,128)(2,1)S(1)}, u32[]{:S(2)}, u32[]{:S(2)}) %collective-permute-start.6) | collective-permute-done | bytes 163872 | tf_op jit(solution)/shard_map/ppermute | solution.py:138
  27.5 0.1 fusion.5
  27.6 0.4 %collective-permute-start.10 = (bf16[16,1280]{1,0:T(8,128)(2,1)S(1)}, bf16[16,1280]{1,0:T(8,128)(2,1)S(1)}, u32[]{:S(2)}, u32[]{:S(2)}) collective-permute-start(bf16[16,1280]{1,0:T(8,128)(2,1)S(1)} %get-tuple-element.23), channel_id=1, source_target_pairs={{0,4},{1,5},{2,6},{3,7},{4,0},{5,1},{6,2},{7,3},{8,12},{9,13},{10,... | collective-permute-start | bytes 122888 | tf_op jit(solution)/shard_map/ppermute | solution.py:25
  28.0 3.1 %collective-permute-start.12 = (bf16[16,1280]{1,0:T(8,128)(2,1)S(1)}, bf16[16,1280]{1,0:T(8,128)(2,1)S(1)}, u32[]{:S(2)}, u32[]{:S(2)}) collective-permute-start(bf16[16,1280]{1,0:T(8,128)(2,1)S(1)} %get-tuple-element.24), channel_id=1, source_target_pairs={{0,12},{1,13},{2,14},{3,15},{4,8},{5,9},{6,10},{7,11},{8,4},{9,5},... | collective-permute-start | bytes 122888 | tf_op jit(solution)/shard_map/ppermute | solution.py:25
  31.2 0.0 collective-permute-start.11
  31.2 0.0 copy-done
  31.2 0.8 %collective-permute-done.10 = bf16[16,1280]{1,0:T(8,128)(2,1)S(1)} collective-permute-done((bf16[16,1280]{1,0:T(8,128)(2,1)S(1)}, bf16[16,1280]{1,0:T(8,128)(2,1)S(1)}, u32[]{:S(2)}, u32[]{:S(2)}) %collective-permute-start.10) | collective-permute-done | bytes 40992 | tf_op jit(solution)/shard_map/ppermute | solution.py:25
  32.0 1.9 %collective-permute-done.12 = bf16[16,1280]{1,0:T(8,128)(2,1)S(1)} collective-permute-done((bf16[16,1280]{1,0:T(8,128)(2,1)S(1)}, bf16[16,1280]{1,0:T(8,128)(2,1)S(1)}, u32[]{:S(2)}, u32[]{:S(2)}) %collective-permute-start.12) | collective-permute-done | bytes 40992 | tf_op jit(solution)/shard_map/ppermute | solution.py:25
  33.8 2.2 %collective-permute-done.11 = bf16[16,1280]{1,0:T(8,128)(2,1)S(1)} collective-permute-done((bf16[16,1280]{1,0:T(8,128)(2,1)S(1)}, bf16[16,1280]{1,0:T(8,128)(2,1)S(1)}, u32[]{:S(2)}, u32[]{:S(2)}) %collective-permute-start.11) | collective-permute-done | bytes 40992 | tf_op jit(solution)/shard_map/ppermute | solution.py:25
  36.1 0.6 %fusion.4 = bf16[1,16,1280]{2,1,0:T(8,128)(2,1)} fusion(bf16[16,1280]{1,0:T(8,128)(2,1)S(1)} %collective-permute-done.12, bf16[16,1280]{1,0:T(8,128)(2,1)S(1)} %collective-permute-done.11, bf16[16,1280]{1,0:T(8,128)(2,1)S(1)} %collective-permute-done.10, f32[64,1280]{1,0:T(8,128)S(1)} %get-tuple-element.22, f32[1280]{0:T(1024)S(1)} %reduce), kind=kLoop, calls=%fused_computation.6 | loop fusion | flops 163840 | bytes 250880 | tf_op jit(solution)/shard_map/broadcast_in_dim | solution.py:171
  (3 shorter events, 0.0 us)
Async XLA Ops:
  0.0 12.3 %copy-start.1 = (f32[1,512]{1,0:T(1,128)S(1)}, f32[1,512]{1,0:T(1,128)}, u32[]{:S(2)}) copy-start(f32[1,512]{1,0:T(1,128)} %refs_2_.1) | copy-start | bytes 6148
  0.0 16.1 %collective-permute-start.5 = (bf16[1,2,512,1280]{3,2,1,0:T(8,128)(2,1)}, bf16[1,2,512,1280]{3,2,1,0:T(8,128)(2,1)S(1)}, u32[]{:S(2)}, u32[]{:S(2)}) collective-permute-start(bf16[1,2,512,1280]{3,2,1,0:T(8,128)(2,1)} %refs_3_.1), channel_id=1, source_target_pairs={{0,1},{1,0},{2,3},{3,2},{4,5},{5,4},{6,7},{7,6},{8,9},{9,8},{10,11... | collective-permute-start | bytes 7864328 | tf_op jit(solution)/shard_map/ppermute | solution.py:25
  0.5 15.6 %collective-permute-start.3 = (bf16[1,1280,512]{2,1,0:T(8,128)(2,1)}, bf16[1,1280,512]{2,1,0:T(8,128)(2,1)S(1)}, u32[]{:S(2)}, u32[]{:S(2)}) collective-permute-start(bf16[1,1280,512]{2,1,0:T(8,128)(2,1)} %refs_1_.1), channel_id=1, source_target_pairs={{0,1},{1,0},{2,3},{3,2},{4,5},{5,4},{6,7},{7,6},{8,9},{9,8},{10,11... | collective-permute-start | bytes 3932168 | tf_op jit(solution)/shard_map/ppermute | solution.py:25
  0.6 7.8 %collective-permute-start.2 = (bf16[16,1280]{1,0:T(8,128)(2,1)}, bf16[16,1280]{1,0:T(8,128)(2,1)S(1)}, u32[]{:S(2)}, u32[]{:S(2)}) collective-permute-start(bf16[16,1280]{1,0:T(8,128)(2,1)} %bitcast.3), channel_id=1, source_target_pairs={{0,12},{1,13},{2,14},{3,15},{4,8},{5,9},{6,10},{7,11},{8,4},{9,5},... | collective-permute-start | bytes 122888 | tf_op jit(solution)/shard_map/ppermute | solution.py:25
  5.6 5.1 %collective-permute-start.1 = (bf16[16,1280]{1,0:T(8,128)(2,1)}, bf16[16,1280]{1,0:T(8,128)(2,1)S(1)}, u32[]{:S(2)}, u32[]{:S(2)}) collective-permute-start(bf16[16,1280]{1,0:T(8,128)(2,1)} %bitcast.4), channel_id=1, source_target_pairs={{0,8},{1,9},{2,10},{3,11},{4,12},{5,13},{6,14},{7,15},{8,0},{9,1},... | collective-permute-start | bytes 122888 | tf_op jit(solution)/shard_map/ppermute | solution.py:25
  5.6 5.1 %collective-permute-start = (bf16[16,1280]{1,0:T(8,128)(2,1)}, bf16[16,1280]{1,0:T(8,128)(2,1)S(1)}, u32[]{:S(2)}, u32[]{:S(2)}) collective-permute-start(bf16[16,1280]{1,0:T(8,128)(2,1)} %bitcast.5), channel_id=1, source_target_pairs={{0,4},{1,5},{2,6},{3,7},{4,0},{5,1},{6,2},{7,3},{8,12},{9,13},{10,... | collective-permute-start | bytes 122888 | tf_op jit(solution)/shard_map/ppermute | solution.py:25
  10.7 5.4 %collective-permute-start.7 = (bf16[64,1280]{1,0:T(8,128)(2,1)S(1)}, bf16[64,1280]{1,0:T(8,128)(2,1)S(1)}, u32[]{:S(2)}, u32[]{:S(2)}) collective-permute-start(bf16[64,1280]{1,0:T(8,128)(2,1)S(1)} %shard_map.56.x), channel_id=1, source_target_pairs={{0,2},{1,3},{2,0},{3,1},{4,6},{5,7},{6,4},{7,5},{8,10},{9,11},{10,... | collective-permute-start | bytes 491528 | tf_op jit(solution)/shard_map/ppermute | solution.py:25
  12.3 1.2 %collective-permute-start.4 = (f32[1,512]{1,0:T(1,128)S(1)}, f32[1,512]{1,0:T(1,128)S(1)}, u32[]{:S(2)}, u32[]{:S(2)}) collective-permute-start(f32[1,512]{1,0:T(1,128)S(1)} %copy-done.1), channel_id=1, source_target_pairs={{0,1},{1,0},{2,3},{3,2},{4,5},{5,4},{6,7},{7,6},{8,9},{9,8},{10,11... | collective-permute-start | bytes 6152 | tf_op jit(solution)/shard_map/ppermute | solution.py:25
  17.3 6.5 %collective-permute-start.8 = (bf16[64,1280]{1,0:T(8,128)(2,1)S(1)}, bf16[64,1280]{1,0:T(8,128)(2,1)S(1)}, u32[]{:S(2)}, u32[]{:S(2)}) collective-permute-start(bf16[64,1280]{1,0:T(8,128)(2,1)S(1)} %get-tuple-element.19), channel_id=1, source_target_pairs={{0,18},{1,19},{2,16},{3,17},{4,22},{5,23},{6,20},{7,21},{8,26},{9,... | collective-permute-start | bytes 491528 | tf_op jit(solution)/shard_map/ppermute | solution.py:138
  19.8 11.4 %copy-start = (f32[1,1280]{1,0:T(1,128)S(1)}, f32[1,1280]{1,0:T(1,128)}, u32[]{:S(2)}) copy-start(f32[1,1280]{1,0:T(1,128)} %param.9) | copy-start | bytes 15364
  19.8 5.4 %collective-permute-start.9 = (bf16[64,1280]{1,0:T(8,128)(2,1)S(1)}, bf16[64,1280]{1,0:T(8,128)(2,1)S(1)}, u32[]{:S(2)}, u32[]{:S(2)}) collective-permute-start(bf16[64,1280]{1,0:T(8,128)(2,1)S(1)} %shard_map.59), channel_id=1, source_target_pairs={{0,2},{1,3},{2,0},{3,1},{4,6},{5,7},{6,4},{7,5},{8,10},{9,11},{10,... | collective-permute-start | bytes 491528 | tf_op jit(solution)/shard_map/ppermute | solution.py:138
  22.2 5.3 %collective-permute-start.6 = (bf16[64,1280]{1,0:T(8,128)(2,1)S(1)}, bf16[64,1280]{1,0:T(8,128)(2,1)S(1)}, u32[]{:S(2)}, u32[]{:S(2)}) collective-permute-start(bf16[64,1280]{1,0:T(8,128)(2,1)S(1)} %get-tuple-element.18), channel_id=1, source_target_pairs={{0,16},{1,17},{2,18},{3,19},{4,20},{5,21},{6,22},{7,23},{8,24},{9,... | collective-permute-start | bytes 491528 | tf_op jit(solution)/shard_map/ppermute | solution.py:138
  27.6 4.4 %collective-permute-start.10 = (bf16[16,1280]{1,0:T(8,128)(2,1)S(1)}, bf16[16,1280]{1,0:T(8,128)(2,1)S(1)}, u32[]{:S(2)}, u32[]{:S(2)}) collective-permute-start(bf16[16,1280]{1,0:T(8,128)(2,1)S(1)} %get-tuple-element.23), channel_id=1, source_target_pairs={{0,4},{1,5},{2,6},{3,7},{4,0},{5,1},{6,2},{7,3},{8,12},{9,13},{10,... | collective-permute-start | bytes 122888 | tf_op jit(solution)/shard_map/ppermute | solution.py:25
  28.0 5.8 %collective-permute-start.12 = (bf16[16,1280]{1,0:T(8,128)(2,1)S(1)}, bf16[16,1280]{1,0:T(8,128)(2,1)S(1)}, u32[]{:S(2)}, u32[]{:S(2)}) collective-permute-start(bf16[16,1280]{1,0:T(8,128)(2,1)S(1)} %get-tuple-element.24), channel_id=1, source_target_pairs={{0,12},{1,13},{2,14},{3,15},{4,8},{5,9},{6,10},{7,11},{8,4},{9,5},... | collective-permute-start | bytes 122888 | tf_op jit(solution)/shard_map/ppermute | solution.py:25
  31.2 4.9 %collective-permute-start.11 = (bf16[16,1280]{1,0:T(8,128)(2,1)S(1)}, bf16[16,1280]{1,0:T(8,128)(2,1)S(1)}, u32[]{:S(2)}, u32[]{:S(2)}) collective-permute-start(bf16[16,1280]{1,0:T(8,128)(2,1)S(1)} %get-tuple-element.25), channel_id=1, source_target_pairs={{0,8},{1,9},{2,10},{3,11},{4,12},{5,13},{6,14},{7,15},{8,0},{9,1},... | collective-permute-start | bytes 122888 | tf_op jit(solution)/shard_map/ppermute | solution.py:25
where the time goes:
time: 36.8 us; the launch traced here: 36.7 us
  waiting for transfers between devices  15.7 us (43%)
  starting transfers between devices  14.4 us (39%)
  Pallas kernels  5.74 us (16%)
  other arithmetic  0.75 us (2%)
    ppermute x10, starting transfers between devices, swap(): return lax.ppermute(x, 'lat', [(i, i ^ k) for i in range(n)])  11.3 us
    ppermute x10, waiting for transfers between devices, swap(): return lax.ppermute(x, 'lat', [(i, i ^ k) for i in range(n)])  11 us
    pallas_call x5, Pallas kernels, call(): pl.pallas_call(kernel, out_shape=outs, in_specs=specs or [VMEM] * len(arg...  5.74 us
    ppermute x3, waiting for transfers between devices, send(): return lax.ppermute(part, ('layer', 'lat'), pairs)  4.73 us
    ppermute x3, starting transfers between devices, send(): return lax.ppermute(part, ('layer', 'lat'), pairs)  3.1 us
  transfers between devices with their start and end apart: 13, of which 9 were waited for; matrix products, arithmetic and copies ran while one was open for 0% of the time, Pallas kernels for 13%

commit v1 on v0

--- a/solution.py
+++ b/solution.py
@@ -19,6 +19,10 @@
     core = min(2, n)
     outer = min(4, n // core)
     return outer, n // core // outer, core
+
+
+def zstep(k, middle, core):
+    return k * middle * core + core - 1
 
 
 def swap(x, n, k):
@@ -79,7 +83,7 @@
         latent[:, c * size : (c + 1) * size] = jnp.maximum(pre, 0.0).astype(BF16)
 
 
-def decode(latent, w_refs, d, layers, out):
+def decode(latent, w_refs, d, layers, outs):
     target = lax.axis_index("layer") + d
 
     @pl.when(target < layers)
@@ -89,25 +93,46 @@
             size = w.shape[2]
             part = jnp.dot(latent[:, c * size : (c + 1) * size], w[0, target], preferred_element_type=F32)
             total = part if total is None else total + part
-        out[...] = total.astype(out.dtype)
+        at = 0
+        for out in outs:
+            out[...] = total[at : at + out.shape[0]].astype(out.dtype)
+            at += out.shape[0]
 
     if d:
 
         @pl.when(target >= layers)
         def _():
-            out[...] = jnp.zeros_like(out)
-
-
-def encode_kernel(core, ds, layers, x, *refs):
+            for out in outs:
+                out[...] = jnp.zeros_like(out)
+
+
+def encode_kernel(core, slots, plan, layers, *refs):
+    xs = 1 + max(at[0] for at in slots)
+    x_refs, refs = refs[:xs], refs[xs:]
     w_refs, b_refs, d_refs = refs[:core], refs[core : 2 * core], refs[2 * core : 3 * core]
-    latent, outs = refs[3 * core], refs[3 * core + 1 :]
+    latent, outs, x = refs[3 * core], refs[3 * core + 1 : -1], refs[-1]
+    at = 0
+    for which, first, rows in slots:
+        x[pl.ds(at, rows), :] = x_refs[which][pl.ds(first, rows), :]
+        at += rows
     encode(x, w_refs, b_refs, latent)
-    for d, out in zip(ds, outs):
-        decode(latent, d_refs, d, layers, out)
+    for d, groups in plan:
+        decode(latent, d_refs, d, layers, outs[:groups])
+        outs = outs[groups:]
 
 
 def decode_kernel(core, layers, latent, *refs):
-    decode(latent, refs[:core], 0, layers, refs[core])
+    decode(latent, refs[:core], 0, layers, refs[core:])
+
+
+def sum_kernel(ats, block, *refs):
+    parts, outs = refs[: len(ats)], refs[len(ats) :]
+    for j, out in enumerate(outs):
+        total = None
+        for at, ref in zip(ats, parts):
+            part = ref[pl.ds(at + j * block, block), :].astype(F32)
+            total = part if total is None else total + part
+        out[...] = total.astype(out.dtype)
 
 
 def work(acts, enc_weight, enc_bias, dec_weight, dec_bias):
@@ -117,17 +142,31 @@
     width = acts.shape[2]
     size = enc_weight.shape[2]
 
-    pieces = [swap(acts[0], n, k * middle * core) for k in range(1, outer)]
+    pieces = [swap(acts[0], n, zstep(k, middle, core)) for k in range(1, outer)]
     enc = [swap(enc_weight, n, k) for k in range(1, core)]
     dec = [swap(dec_weight, n, k) for k in range(1, core)]
     bias = [swap(enc_bias, n, k) for k in range(1, core)]
     own, own_enc, own_bias, own_dec = load(acts[0], enc_weight, enc_bias, dec_weight)
     enc, dec, bias = [own_enc] + enc, [own_dec] + dec, [own_bias] + bias
-    column = stack([own] + pieces)
-    xs = [column] + [swap(column, n, k * core) for k in range(1, middle)]
-    rows = column.shape[0]
+    block = own.shape[0]
+    rows = block * outer
     flops = 2 * rows * core * size * width
     hidden = jax.ShapeDtypeStruct((rows, core * size), BF16)
+
+    blocks = [own] + pieces
+    batches = [[0] + list(range(outer - 1, 0, -1))[:1], list(range(1, outer - 1))]
+    batches = [batch for batch in batches if batch]
+    stacks = [stack([blocks[k] for k in batch]) for batch in batches]
+    slots = [None] * outer
+    for i, batch in enumerate(batches):
+        for j, k in enumerate(batch):
+            slots[k] = (i, j * block, block)
+    xs = [(blocks, [(k, 0, block) for k in range(outer)])]
+    for k in range(1, middle):
+        xs.append(([swap(x, n, k * core) for x in stacks], slots))
+
+    groups = cuts(outer)
+    order = [k for group in groups for k in group]
 
     def send(part, d, k):
         pairs = [
@@ -137,38 +176,64 @@
         ]
         return lax.ppermute(part, ("layer", "lat"), pairs)
 
-    received = []
-    total = None
+    def shapes(dtype, whole=False):
+        sizes = [rows] if whole else [block * len(group) for group in groups]
+        return [jax.ShapeDtypeStruct((size, width), dtype) for size in sizes]
+
+    totals = [[] for _ in groups]
     later = list(range(layers - 1, 0, -1))
-    for k, x in enumerate(xs):
-        ds = later if k else later + [0]
-        outs = [jax.ShapeDtypeStruct((rows, width), BF16 if d else F32) for d in ds]
+    for k, (x, where) in enumerate(xs):
+        plan = [(d, len(groups) if k else 1) for d in later] + ([] if k else [(0, len(groups))])
+        outs = [shape for d, _ in plan for shape in shapes(BF16 if d else F32, d > 0 and k == 0)]
         latent, *parts = call(
-            functools.partial(encode_kernel, core, ds, layers),
+            functools.partial(encode_kernel, core, [where[j] for j in order], plan, layers),
             [hidden] + outs,
-            [x] + enc + bias + dec,
-            flops=flops * (1 + len(ds)),
+            x + enc + bias + dec,
+            scratch=[pltpu.VMEM((rows, width), BF16)],
+            flops=flops * (1 + len(plan)),
         )
-        for d, part in zip(ds, parts):
-            if d:
-                received.append(send(part, d, k))
-            else:
-                total = part
-        if k:
-            part = call(
+        if k == 0:
+            for d in later:
+                got = send(parts.pop(0), d, k)
+                at = 0
+                for total, group in zip(totals, groups):
+                    total.append((at, got))
+                    at += block * len(group)
+            for total in totals:
+                total.insert(0, (0, parts.pop(0)))
+        else:
+            own_parts = call(
                 functools.partial(decode_kernel, core, layers),
-                [jax.ShapeDtypeStruct((rows, width), BF16)],
+                shapes(BF16),
                 [latent] + dec,
                 flops=flops,
-            )[0]
-            received.append(send(part, 0, k))
-    for piece in received:
-        total = total + piece.astype(F32)
-    pieces = total.reshape(outer, -1, width)
-    total = pieces[0]
-    for k in range(1, outer):
-        total = total + swap(pieces[k].astype(BF16), n, k * middle * core).astype(F32)
-    return (total + dec_bias[0][None, :]).astype(BF16)[None]
+            )
+            for g, total in enumerate(totals):
+                for i, d in enumerate(later):
+                    total.append((0, send(parts[i * len(groups) + g], d, k)))
+                total.append((0, send(own_parts[g], 0, k)))
+    result = None
+    near = []
+    for total, group in zip(totals, groups):
+        pieces = call(
+            functools.partial(sum_kernel, [at for at, _ in total], block),
+            [jax.ShapeDtypeStruct((block, width), BF16 if k else F32) for k in group],
+            [part for _, part in total],
+        )
+        for k, piece in zip(group, pieces):
+            if k:
+                near.append(swap(piece, n, zstep(k, middle, core)))
+            else:
+                result = piece
+    for piece in near:
+        result = result + piece.astype(F32)
+    return (result + dec_bias[0][None, :]).astype(BF16)[None]
+
+
+def cuts(outer):
+    far = list(range(outer - 1, 0, -1))
+    half = len(far) - max(outer // 2 - 1, 0)
+    return [group for group in (far[:half], far[half:] + [0]) if group]
 
 
 def solution(mesh):

time: 36.8 us -> 35.3 us (0.959)
  waiting for transfers between devices: 15.7 us -> 10.8 us
  starting transfers between devices: 14.4 us -> 17.8 us
    ppermute x3 -> x5, starting transfers between devices: 3.1 us -> 6.17 us  [send(): return lax.ppermute(part, ('layer', 'lat'), pairs)]
    ppermute x10 -> x11, waiting for transfers between devices: 11 us -> 8.06 us  [swap(): return lax.ppermute(x, 'lat', [(i, i ^ k) for i in range(n)])]
    ppermute x3 -> x5, waiting for transfers between devices: 4.73 us -> 2.75 us  [send(): return lax.ppermute(part, ('layer', 'lat'), pairs)]
    ppermute x10 -> x11, starting transfers between devices: 11.3 us -> 11.6 us  [swap(): return lax.ppermute(x, 'lat', [(i, i ^ k) for i in range(n)])]
    pallas_call x5 -> x8, Pallas kernels: 5.74 us -> 5.82 us  [call(): pl.pallas_call(kernel, out_shape=outs, in_specs=specs or [VMEM] * len(arg...]
  transfers between devices with their start and end apart: 13 -> 16, of which waited for: 9 -> 7; matrix products, arithmetic and copies ran while one was open for 0% -> 0% of each run, Pallas kernels for 13% -> 17%
where the time goes in v1:
time: 35.3 us; the launch traced here: 35.1 us
  starting transfers between devices  17.8 us (50%)
  waiting for transfers between devices  10.8 us (31%)
  Pallas kernels  5.82 us (16%)
  other arithmetic  0.67 us (2%)
    ppermute x11, starting transfers between devices, swap(): return lax.ppermute(x, 'lat', [(i, i ^ k) for i in range(n)])  11.6 us
    ppermute x11, waiting for transfers between devices, swap(): return lax.ppermute(x, 'lat', [(i, i ^ k) for i in range(n)])  8.06 us
    ppermute x5, starting transfers between devices, send(): return lax.ppermute(part, ('layer', 'lat'), pairs)  6.17 us
    pallas_call x8, Pallas kernels, call(): pl.pallas_call(kernel, out_shape=outs, in_specs=specs or [VMEM] * len(arg...  5.82 us
    ppermute x5, waiting for transfers between devices, send(): return lax.ppermute(part, ('layer', 'lat'), pairs)  2.75 us
  transfers between devices with their start and end apart: 16, of which 7 were waited for; matrix products, arithmetic and copies ran while one was open for 0% of the time, Pallas kernels for 17%

profile of v1, /device:TPU:0, one launch (start us, length us, event | category | flops | bytes accessed | tf_op | source)
XLA Modules:
  0.0 35.1 jit_solution(8179786650317516537)
XLA Ops:
  0.0 0.5 %collective-permute-start.5 = (bf16[1,2,512,1280]{3,2,1,0:T(8,128)(2,1)}, bf16[1,2,512,1280]{3,2,1,0:T(8,128)(2,1)S(1)}, u32[]{:S(2)}, u32[]{:S(2)}) collective-permute-start(bf16[1,2,512,1280]{3,2,1,0:T(8,128)(2,1)} %refs_3_.1), channel_id=1, source_target_pairs={{0,1},{1,0},{2,3},{3,2},{4,5},{5,4},{6,7},{7,6},{8,9},{9,8},{10,11... | collective-permute-start | bytes 7864328 | tf_op jit(solution)/shard_map/ppermute | solution.py:29
  0.5 0.0 collective-permute-start.3
  0.5 4.7 %collective-permute-start.2 = (bf16[16,1280]{1,0:T(8,128)(2,1)}, bf16[16,1280]{1,0:T(8,128)(2,1)S(1)}, u32[]{:S(2)}, u32[]{:S(2)}) collective-permute-start(bf16[16,1280]{1,0:T(8,128)(2,1)} %bitcast.3), channel_id=1, source_target_pairs={{0,13},{1,12},{2,15},{3,14},{4,9},{5,8},{6,11},{7,10},{8,5},{9,4},... | collective-permute-start | bytes 122888 | tf_op jit(solution)/shard_map/ppermute | solution.py:29
  5.2 0.0 collective-permute-start
  5.2 0.7 %collective-permute-start.1 = (bf16[16,1280]{1,0:T(8,128)(2,1)}, bf16[16,1280]{1,0:T(8,128)(2,1)S(1)}, u32[]{:S(2)}, u32[]{:S(2)}) collective-permute-start(bf16[16,1280]{1,0:T(8,128)(2,1)} %bitcast.5), channel_id=1, source_target_pairs={{0,9},{1,8},{2,11},{3,10},{4,13},{5,12},{6,15},{7,14},{8,1},{9,0},... | collective-permute-start | bytes 122888 | tf_op jit(solution)/shard_map/ppermute | solution.py:29
  5.9 1.6 %collective-permute-done.2.refs_3_.refs_1_ = bf16[16,1280]{1,0:T(8,128)(2,1)S(1)} collective-permute-done((bf16[16,1280]{1,0:T(8,128)(2,1)}, bf16[16,1280]{1,0:T(8,128)(2,1)S(1)}, u32[]{:S(2)}, u32[]{:S(2)}) %collective-permute-start.2) | collective-permute-done | bytes 40992 | tf_op jit(solution)/shard_map/ppermute | solution.py:29
  7.5 0.5 %collective-permute-start.4 = (f32[1,512]{1,0:T(1,128)}, f32[1,512]{1,0:T(1,128)S(1)}, u32[]{:S(2)}, u32[]{:S(2)}) collective-permute-start(f32[1,512]{1,0:T(1,128)} %refs_2_.1), channel_id=1, source_target_pairs={{0,1},{1,0},{2,3},{3,2},{4,5},{5,4},{6,7},{7,6},{8,9},{9,8},{10,11... | collective-permute-start | bytes 6152 | tf_op jit(solution)/shard_map/ppermute | solution.py:29
  8.0 2.2 %shard_map.55 = (bf16[16,1280]{1,0:T(8,128)(2,1)S(1)}, bf16[1,1280,512]{2,1,0:T(8,128)(2,1)S(1)}, f32[1,512]{1,0:T(1,128)S(1)}, bf16[1,2,512,1280]{3,2,1,0:T(8,128)(2,1)S(1)}) custom-call(bf16[16,1280]{1,0:T(8,128)(2,1)} %bitcast.6, bf16[1,1280,512]{2,1,0:T(8,128)(2,1)} %refs_1_.1, f32[1,512]{1,0:T(1,128)} %refs_2_.1, bf16[1,2,512,1280]{3,2,1,0:T(8,128)(2,1)} %refs_3_.1), custom_call_target="tpu_custom_call" | custom-call | flops 1000000 | bytes 1048576 | tf_op jit(solution)/shard_map/pallas_call | solution.py:33
  10.2 0.0 collective-permute-done.refs_1_.refs_0_
  10.2 1.7 %collective-permute-start.7 = (bf16[32,1280]{1,0:T(8,128)(2,1)S(1)}, bf16[32,1280]{1,0:T(8,128)(2,1)S(1)}, u32[]{:S(2)}, u32[]{:S(2)}) collective-permute-start(bf16[32,1280]{1,0:T(8,128)(2,1)S(1)} %shard_map.57), channel_id=1, source_target_pairs={{0,2},{1,3},{2,0},{3,1},{4,6},{5,7},{6,4},{7,5},{8,10},{9,11},{10,... | collective-permute-start | bytes 245768 | tf_op jit(solution)/shard_map/ppermute | solution.py:29
  11.9 0.0 collective-permute-done.1.refs_2_.refs_1_
  11.9 0.5 %collective-permute-start.8 = (bf16[32,1280]{1,0:T(8,128)(2,1)S(1)}, bf16[32,1280]{1,0:T(8,128)(2,1)S(1)}, u32[]{:S(2)}, u32[]{:S(2)}) collective-permute-start(bf16[32,1280]{1,0:T(8,128)(2,1)S(1)} %shard_map.58), channel_id=1, source_target_pairs={{0,2},{1,3},{2,0},{3,1},{4,6},{5,7},{6,4},{7,5},{8,10},{9,11},{10,... | collective-permute-start | bytes 245768 | tf_op jit(solution)/shard_map/ppermute | solution.py:29
  12.4 0.0 collective-permute-done.4.refs_7_.refs_5_
  12.4 0.0 collective-permute-done.3.refs_5_.refs_3_
  12.4 0.0 collective-permute-done.5.refs_9_.refs_7_.refs_1_
  12.4 1.8 %shard_map.56 = (bf16[64,1024]{1,0:T(8,128)(2,1)}, bf16[64,1280]{1,0:T(8,128)(2,1)S(1)}, f32[32,1280]{1,0:T(8,128)S(1)}, f32[32,1280]{1,0:T(8,128)S(1)}) custom-call(bf16[16,1280]{1,0:T(8,128)(2,1)S(1)} %get-tuple-element.21.refs_0_, bf16[16,1280]{1,0:T(8,128)(2,1)S(1)} %collective-permute-done.refs_1_.refs_0_, ...), custom_call_target="tpu_custom_call" | custom-call | flops 503316480 | bytes 1048576 | tf_op jit(solution)/shard_map/pallas_call | solution.py:33
  14.2 1.0 %collective-permute-start.6 = (bf16[64,1280]{1,0:T(8,128)(2,1)S(1)}, bf16[64,1280]{1,0:T(8,128)(2,1)S(1)}, u32[]{:S(2)}, u32[]{:S(2)}) collective-permute-start(bf16[64,1280]{1,0:T(8,128)(2,1)S(1)} %get-tuple-element.26), channel_id=1, source_target_pairs={{0,16},{1,17},{2,18},{3,19},{4,20},{5,21},{6,22},{7,23},{8,24},{9,... | collective-permute-start | bytes 491528 | tf_op jit(solution)/shard_map/ppermute | solution.py:177
  15.2 0.0 collective-permute-done.7.refs_0_
  15.2 1.3 %collective-permute-done.8.refs_1_ = bf16[32,1280]{1,0:T(8,128)(2,1)S(1)} collective-permute-done((bf16[32,1280]{1,0:T(8,128)(2,1)S(1)}, bf16[32,1280]{1,0:T(8,128)(2,1)S(1)}, u32[]{:S(2)}, u32[]{:S(2)}) %collective-permute-start.8) | collective-permute-done | bytes 81952 | tf_op jit(solution)/shard_map/ppermute | solution.py:29
  16.5 1.1 %shard_map.59 = (bf16[64,1024]{1,0:T(8,128)(2,1)S(1)}, bf16[32,1280]{1,0:T(8,128)(2,1)S(1)}, bf16[32,1280]{1,0:T(8,128)(2,1)S(1)}) custom-call(bf16[32,1280]{1,0:T(8,128)(2,1)S(1)} %collective-permute-done.7.refs_0_, bf16[32,1280]{1,0:T(8,128)(2,1)S(1)} %collective-permute-done.8.refs_1_, bf16[1,1280,512]{2,1,0:T(8,128)(2,1)S(1)} %get-tuple-element.22.refs_4_.refs_2_, ...), custom_call_target="tpu_custom_call" | custom-call | flops 335544320 | bytes 1048576 | tf_op jit(solution)/shard_map/pallas_call | solution.py:33
  17.6 2.0 %collective-permute-start.9 = (bf16[32,1280]{1,0:T(8,128)(2,1)S(1)}, bf16[32,1280]{1,0:T(8,128)(2,1)S(1)}, u32[]{:S(2)}, u32[]{:S(2)}) collective-permute-start(bf16[32,1280]{1,0:T(8,128)(2,1)S(1)} %get-tuple-element.27), channel_id=1, source_target_pairs={{0,18},{1,19},{2,16},{3,17},{4,22},{5,23},{6,20},{7,21},{8,26},{9,... | collective-permute-start | bytes 245768 | tf_op jit(solution)/shard_map/ppermute | solution.py:177
  19.6 0.0 copy-start
  19.6 0.6 %shard_map.60 = (bf16[32,1280]{1,0:T(8,128)(2,1)S(1)}, bf16[32,1280]{1,0:T(8,128)(2,1)S(1)}) custom-call(bf16[64,1024]{1,0:T(8,128)(2,1)S(1)} %get-tuple-element.28.latent, bf16[1,2,512,1280]{3,2,1,0:T(8,128)(2,1)S(1)} %get-tuple-element.24.refs_8_.refs_6_.refs_0_, bf16[1,2,512,1280]{3,2,1,0:T(8,128)(2,1)S(1)} %collective-permute-done.5.refs_9_.refs_7_.refs_1_), custom_call_target="tpu_custom_call" | custom-call | flops 167772160 | bytes 1048576 | tf_op jit(solution)/shard_map/pallas_call | solution.py:33
  20.2 0.6 %collective-permute-start.10 = (bf16[32,1280]{1,0:T(8,128)(2,1)S(1)}, bf16[32,1280]{1,0:T(8,128)(2,1)S(1)}, u32[]{:S(2)}, u32[]{:S(2)}) collective-permute-start(bf16[32,1280]{1,0:T(8,128)(2,1)S(1)} %get-tuple-element.29), channel_id=1, source_target_pairs={{0,2},{1,3},{2,0},{3,1},{4,6},{5,7},{6,4},{7,5},{8,10},{9,11},{10,... | collective-permute-start | bytes 245768 | tf_op jit(solution)/shard_map/ppermute | solution.py:177
  20.8 1.0 %collective-permute-start.11 = (bf16[32,1280]{1,0:T(8,128)(2,1)S(1)}, bf16[32,1280]{1,0:T(8,128)(2,1)S(1)}, u32[]{:S(2)}, u32[]{:S(2)}) collective-permute-start(bf16[32,1280]{1,0:T(8,128)(2,1)S(1)} %get-tuple-element.32), channel_id=1, source_target_pairs={{0,18},{1,19},{2,16},{3,17},{4,22},{5,23},{6,20},{7,21},{8,26},{9,... | collective-permute-start | bytes 245768 | tf_op jit(solution)/shard_map/ppermute | solution.py:177
  21.8 1.6 %collective-permute-start.12 = (bf16[32,1280]{1,0:T(8,128)(2,1)S(1)}, bf16[32,1280]{1,0:T(8,128)(2,1)S(1)}, u32[]{:S(2)}, u32[]{:S(2)}) collective-permute-start(bf16[32,1280]{1,0:T(8,128)(2,1)S(1)} %get-tuple-element.33), channel_id=1, source_target_pairs={{0,2},{1,3},{2,0},{3,1},{4,6},{5,7},{6,4},{7,5},{8,10},{9,11},{10,... | collective-permute-start | bytes 245768 | tf_op jit(solution)/shard_map/ppermute | solution.py:177
  23.4 0.0 collective-permute-done.9.refs_2_
  23.4 1.3 %collective-permute-done.10.refs_3_ = bf16[32,1280]{1,0:T(8,128)(2,1)S(1)} collective-permute-done((bf16[32,1280]{1,0:T(8,128)(2,1)S(1)}, bf16[32,1280]{1,0:T(8,128)(2,1)S(1)}, u32[]{:S(2)}, u32[]{:S(2)}) %collective-permute-start.10) | collective-permute-done | bytes 81952 | tf_op jit(solution)/shard_map/ppermute | solution.py:177
  24.7 0.0 collective-permute-done.6.refs_1_
  24.7 0.1 collective-permute-start.15
  24.8 0.4 %collective-permute-done.11.refs_2_ = bf16[32,1280]{1,0:T(8,128)(2,1)S(1)} collective-permute-done((bf16[32,1280]{1,0:T(8,128)(2,1)S(1)}, bf16[32,1280]{1,0:T(8,128)(2,1)S(1)}, u32[]{:S(2)}, u32[]{:S(2)}) %collective-permute-start.11) | collective-permute-done | bytes 81952 | tf_op jit(solution)/shard_map/ppermute | solution.py:177
  25.2 1.0 %collective-permute-done.12.refs_3_ = bf16[32,1280]{1,0:T(8,128)(2,1)S(1)} collective-permute-done((bf16[32,1280]{1,0:T(8,128)(2,1)S(1)}, bf16[32,1280]{1,0:T(8,128)(2,1)S(1)}, u32[]{:S(2)}, u32[]{:S(2)}) %collective-permute-start.12) | collective-permute-done | bytes 81952 | tf_op jit(solution)/shard_map/ppermute | solution.py:177
  26.3 3.0 %collective-permute-start.14 = (bf16[16,1280]{1,0:T(8,128)(2,1)S(1)}, bf16[16,1280]{1,0:T(8,128)(2,1)S(1)}, u32[]{:S(2)}, u32[]{:S(2)}) collective-permute-start(bf16[16,1280]{1,0:T(8,128)(2,1)S(1)} %get-tuple-element.35), channel_id=1, source_target_pairs={{0,9},{1,8},{2,11},{3,10},{4,13},{5,12},{6,15},{7,14},{8,1},{9,0},... | collective-permute-start | bytes 122888 | tf_op jit(solution)/shard_map/ppermute | solution.py:29
  29.3 0.0 collective-permute-start.13
  29.3 0.0 copy-done
  29.3 0.0 collective-permute-done.15
  29.3 1.6 %collective-permute-done.14 = bf16[16,1280]{1,0:T(8,128)(2,1)S(1)} collective-permute-done((bf16[16,1280]{1,0:T(8,128)(2,1)S(1)}, bf16[16,1280]{1,0:T(8,128)(2,1)S(1)}, u32[]{:S(2)}, u32[]{:S(2)}) %collective-permute-start.14) | collective-permute-done | bytes 40992 | tf_op jit(solution)/shard_map/ppermute | solution.py:29
  31.0 3.5 %collective-permute-done.13 = bf16[16,1280]{1,0:T(8,128)(2,1)S(1)} collective-permute-done((bf16[16,1280]{1,0:T(8,128)(2,1)S(1)}, bf16[16,1280]{1,0:T(8,128)(2,1)S(1)}, u32[]{:S(2)}, u32[]{:S(2)}) %collective-permute-start.13) | collective-permute-done | bytes 40992 | tf_op jit(solution)/shard_map/ppermute | solution.py:29
  34.5 0.6 %fusion = bf16[1,16,1280]{2,1,0:T(8,128)(2,1)} fusion(bf16[16,1280]{1,0:T(8,128)(2,1)S(1)} %collective-permute-done.15, bf16[16,1280]{1,0:T(8,128)(2,1)S(1)} %collective-permute-done.14, f32[16,1280]{1,0:T(8,128)S(1)} %get-tuple-element.30, bf16[16,1280]{1,0:T(8,128)(2,1)S(1)} %collective-permute-done.13, f32[1280]{0:T(1024)S(1)} %reduce), kind=kLoop, calls=%fused_computation.1 | loop fusion | flops 163840 | bytes 250880 | tf_op jit(solution)/shard_map/broadcast_in_dim | solution.py:230
  (5 shorter events, 0.1 us)
Async XLA Ops:
  0.0 12.4 %collective-permute-start.5 = (bf16[1,2,512,1280]{3,2,1,0:T(8,128)(2,1)}, bf16[1,2,512,1280]{3,2,1,0:T(8,128)(2,1)S(1)}, u32[]{:S(2)}, u32[]{:S(2)}) collective-permute-start(bf16[1,2,512,1280]{3,2,1,0:T(8,128)(2,1)} %refs_3_.1), channel_id=1, source_target_pairs={{0,1},{1,0},{2,3},{3,2},{4,5},{5,4},{6,7},{7,6},{8,9},{9,8},{10,11... | collective-permute-start | bytes 7864328 | tf_op jit(solution)/shard_map/ppermute | solution.py:29
  0.5 11.9 %collective-permute-start.3 = (bf16[1,1280,512]{2,1,0:T(8,128)(2,1)}, bf16[1,1280,512]{2,1,0:T(8,128)(2,1)S(1)}, u32[]{:S(2)}, u32[]{:S(2)}) collective-permute-start(bf16[1,1280,512]{2,1,0:T(8,128)(2,1)} %refs_1_.1), channel_id=1, source_target_pairs={{0,1},{1,0},{2,3},{3,2},{4,5},{5,4},{6,7},{7,6},{8,9},{9,8},{10,11... | collective-permute-start | bytes 3932168 | tf_op jit(solution)/shard_map/ppermute | solution.py:29
  0.5 7.0 %collective-permute-start.2 = (bf16[16,1280]{1,0:T(8,128)(2,1)}, bf16[16,1280]{1,0:T(8,128)(2,1)S(1)}, u32[]{:S(2)}, u32[]{:S(2)}) collective-permute-start(bf16[16,1280]{1,0:T(8,128)(2,1)} %bitcast.3), channel_id=1, source_target_pairs={{0,13},{1,12},{2,15},{3,14},{4,9},{5,8},{6,11},{7,10},{8,5},{9,4},... | collective-permute-start | bytes 122888 | tf_op jit(solution)/shard_map/ppermute | solution.py:29
  5.2 5.0 %collective-permute-start = (bf16[16,1280]{1,0:T(8,128)(2,1)}, bf16[16,1280]{1,0:T(8,128)(2,1)S(1)}, u32[]{:S(2)}, u32[]{:S(2)}) collective-permute-start(bf16[16,1280]{1,0:T(8,128)(2,1)} %bitcast.4), channel_id=1, source_target_pairs={{0,5},{1,4},{2,7},{3,6},{4,1},{5,0},{6,3},{7,2},{8,13},{9,12},{10,... | collective-permute-start | bytes 122888 | tf_op jit(solution)/shard_map/ppermute | solution.py:29
  5.2 6.7 %collective-permute-start.1 = (bf16[16,1280]{1,0:T(8,128)(2,1)}, bf16[16,1280]{1,0:T(8,128)(2,1)S(1)}, u32[]{:S(2)}, u32[]{:S(2)}) collective-permute-start(bf16[16,1280]{1,0:T(8,128)(2,1)} %bitcast.5), channel_id=1, source_target_pairs={{0,9},{1,8},{2,11},{3,10},{4,13},{5,12},{6,15},{7,14},{8,1},{9,0},... | collective-permute-start | bytes 122888 | tf_op jit(solution)/shard_map/ppermute | solution.py:29
  7.5 4.9 %collective-permute-start.4 = (f32[1,512]{1,0:T(1,128)}, f32[1,512]{1,0:T(1,128)S(1)}, u32[]{:S(2)}, u32[]{:S(2)}) collective-permute-start(f32[1,512]{1,0:T(1,128)} %refs_2_.1), channel_id=1, source_target_pairs={{0,1},{1,0},{2,3},{3,2},{4,5},{5,4},{6,7},{7,6},{8,9},{9,8},{10,11... | collective-permute-start | bytes 6152 | tf_op jit(solution)/shard_map/ppermute | solution.py:29
  10.2 5.0 %collective-permute-start.7 = (bf16[32,1280]{1,0:T(8,128)(2,1)S(1)}, bf16[32,1280]{1,0:T(8,128)(2,1)S(1)}, u32[]{:S(2)}, u32[]{:S(2)}) collective-permute-start(bf16[32,1280]{1,0:T(8,128)(2,1)S(1)} %shard_map.57), channel_id=1, source_target_pairs={{0,2},{1,3},{2,0},{3,1},{4,6},{5,7},{6,4},{7,5},{8,10},{9,11},{10,... | collective-permute-start | bytes 245768 | tf_op jit(solution)/shard_map/ppermute | solution.py:29
  11.9 4.6 %collective-permute-start.8 = (bf16[32,1280]{1,0:T(8,128)(2,1)S(1)}, bf16[32,1280]{1,0:T(8,128)(2,1)S(1)}, u32[]{:S(2)}, u32[]{:S(2)}) collective-permute-start(bf16[32,1280]{1,0:T(8,128)(2,1)S(1)} %shard_map.58), channel_id=1, source_target_pairs={{0,2},{1,3},{2,0},{3,1},{4,6},{5,7},{6,4},{7,5},{8,10},{9,11},{10,... | collective-permute-start | bytes 245768 | tf_op jit(solution)/shard_map/ppermute | solution.py:29
  14.2 10.5 %collective-permute-start.6 = (bf16[64,1280]{1,0:T(8,128)(2,1)S(1)}, bf16[64,1280]{1,0:T(8,128)(2,1)S(1)}, u32[]{:S(2)}, u32[]{:S(2)}) collective-permute-start(bf16[64,1280]{1,0:T(8,128)(2,1)S(1)} %get-tuple-element.26), channel_id=1, source_target_pairs={{0,16},{1,17},{2,18},{3,19},{4,20},{5,21},{6,22},{7,23},{8,24},{9,... | collective-permute-start | bytes 491528 | tf_op jit(solution)/shard_map/ppermute | solution.py:177
  17.6 5.8 %collective-permute-start.9 = (bf16[32,1280]{1,0:T(8,128)(2,1)S(1)}, bf16[32,1280]{1,0:T(8,128)(2,1)S(1)}, u32[]{:S(2)}, u32[]{:S(2)}) collective-permute-start(bf16[32,1280]{1,0:T(8,128)(2,1)S(1)} %get-tuple-element.27), channel_id=1, source_target_pairs={{0,18},{1,19},{2,16},{3,17},{4,22},{5,23},{6,20},{7,21},{8,26},{9,... | collective-permute-start | bytes 245768 | tf_op jit(solution)/shard_map/ppermute | solution.py:177
  19.6 9.7 %copy-start = (f32[1,1280]{1,0:T(1,128)S(1)}, f32[1,1280]{1,0:T(1,128)}, u32[]{:S(2)}) copy-start(f32[1,1280]{1,0:T(1,128)} %param.9) | copy-start | bytes 15364
  20.2 4.5 %collective-permute-start.10 = (bf16[32,1280]{1,0:T(8,128)(2,1)S(1)}, bf16[32,1280]{1,0:T(8,128)(2,1)S(1)}, u32[]{:S(2)}, u32[]{:S(2)}) collective-permute-start(bf16[32,1280]{1,0:T(8,128)(2,1)S(1)} %get-tuple-element.29), channel_id=1, source_target_pairs={{0,2},{1,3},{2,0},{3,1},{4,6},{5,7},{6,4},{7,5},{8,10},{9,11},{10,... | collective-permute-start | bytes 245768 | tf_op jit(solution)/shard_map/ppermute | solution.py:177
  20.8 4.4 %collective-permute-start.11 = (bf16[32,1280]{1,0:T(8,128)(2,1)S(1)}, bf16[32,1280]{1,0:T(8,128)(2,1)S(1)}, u32[]{:S(2)}, u32[]{:S(2)}) collective-permute-start(bf16[32,1280]{1,0:T(8,128)(2,1)S(1)} %get-tuple-element.32), channel_id=1, source_target_pairs={{0,18},{1,19},{2,16},{3,17},{4,22},{5,23},{6,20},{7,21},{8,26},{9,... | collective-permute-start | bytes 245768 | tf_op jit(solution)/shard_map/ppermute | solution.py:177
  21.8 4.4 %collective-permute-start.12 = (bf16[32,1280]{1,0:T(8,128)(2,1)S(1)}, bf16[32,1280]{1,0:T(8,128)(2,1)S(1)}, u32[]{:S(2)}, u32[]{:S(2)}) collective-permute-start(bf16[32,1280]{1,0:T(8,128)(2,1)S(1)} %get-tuple-element.33), channel_id=1, source_target_pairs={{0,2},{1,3},{2,0},{3,1},{4,6},{5,7},{6,4},{7,5},{8,10},{9,11},{10,... | collective-permute-start | bytes 245768 | tf_op jit(solution)/shard_map/ppermute | solution.py:177
  24.7 4.6 %collective-permute-start.15 = (bf16[16,1280]{1,0:T(8,128)(2,1)S(1)}, bf16[16,1280]{1,0:T(8,128)(2,1)S(1)}, u32[]{:S(2)}, u32[]{:S(2)}) collective-permute-start(bf16[16,1280]{1,0:T(8,128)(2,1)S(1)} %get-tuple-element.36), channel_id=1, source_target_pairs={{0,5},{1,4},{2,7},{3,6},{4,1},{5,0},{6,3},{7,2},{8,13},{9,12},{10,... | collective-permute-start | bytes 122888 | tf_op jit(solution)/shard_map/ppermute | solution.py:29
  26.3 4.7 %collective-permute-start.14 = (bf16[16,1280]{1,0:T(8,128)(2,1)S(1)}, bf16[16,1280]{1,0:T(8,128)(2,1)S(1)}, u32[]{:S(2)}, u32[]{:S(2)}) collective-permute-start(bf16[16,1280]{1,0:T(8,128)(2,1)S(1)} %get-tuple-element.35), channel_id=1, source_target_pairs={{0,9},{1,8},{2,11},{3,10},{4,13},{5,12},{6,15},{7,14},{8,1},{9,0},... | collective-permute-start | bytes 122888 | tf_op jit(solution)/shard_map/ppermute | solution.py:29
  29.3 5.2 %collective-permute-start.13 = (bf16[16,1280]{1,0:T(8,128)(2,1)S(1)}, bf16[16,1280]{1,0:T(8,128)(2,1)S(1)}, u32[]{:S(2)}, u32[]{:S(2)}) collective-permute-start(bf16[16,1280]{1,0:T(8,128)(2,1)S(1)} %get-tuple-element.34), channel_id=1, source_target_pairs={{0,13},{1,12},{2,15},{3,14},{4,9},{5,8},{6,11},{7,10},{8,5},{9,4},... | collective-permute-start | bytes 122888 | tf_op jit(solution)/shard_map/ppermute | solution.py:29

commit v2 on v1

--- a/solution.py
+++ b/solution.py
@@ -41,24 +41,32 @@
     )(*args)
 
 
-def load_kernel(count, *refs):
+def load_kernel(count, ds, layers, *refs):
     sems = refs[2 * count]
-    copies = [pltpu.make_async_copy(refs[i], refs[count + i], sems.at[i]) for i in range(count)]
+    pairs = [(refs[i], refs[count + i]) for i in range(count)]
+    if ds:
+        source, dest = pairs.pop()
+        layer = lax.axis_index("layer")
+        pairs += [(source.at[0, lax.rem(layer + d, layers)], dest.at[0, j]) for j, d in enumerate(ds)]
+    copies = [pltpu.make_async_copy(source, dest, sems.at[i]) for i, (source, dest) in enumerate(pairs)]
     for copy in copies:
         copy.start()
     for copy in copies:
         copy.wait()
 
 
-def load(*arrays):
+def load(arrays, ds=(), layers=1):
     arrays = [pltpu.with_memory_space_constraint(a, pltpu.HBM) for a in arrays]
+    shapes = [a.shape for a in arrays]
+    if ds:
+        shapes[-1] = (1, len(ds)) + shapes[-1][2:]
     count = len(arrays)
     return call(
-        functools.partial(load_kernel, count),
-        [jax.ShapeDtypeStruct(a.shape, a.dtype) for a in arrays],
+        functools.partial(load_kernel, count, tuple(ds), layers),
+        [jax.ShapeDtypeStruct(shape, a.dtype) for shape, a in zip(shapes, arrays)],
         arrays,
         specs=[HBM] * count,
-        scratch=[pltpu.SemaphoreType.DMA((count,))],
+        scratch=[pltpu.SemaphoreType.DMA((count + len(ds),))],
     )
 
 
@@ -91,7 +99,11 @@
         total = None
         for c, w in enumerate(w_refs):
             size = w.shape[2]
-            part = jnp.dot(latent[:, c * size : (c + 1) * size], w[0, target], preferred_element_type=F32)
+            part = jnp.dot(
+                latent[:, c * size : (c + 1) * size],
+                w[0, target if c else max(d - 1, 0)],
+                preferred_element_type=F32,
+            )
             total = part if total is None else total + part
         at = 0
         for out in outs:
@@ -146,7 +158,13 @@
     enc = [swap(enc_weight, n, k) for k in range(1, core)]
     dec = [swap(dec_weight, n, k) for k in range(1, core)]
     bias = [swap(enc_bias, n, k) for k in range(1, core)]
-    own, own_enc, own_bias, own_dec = load(acts[0], enc_weight, enc_bias, dec_weight)
+    later = list(range(layers - 1, 0, -1))
+    ahead = later[::-1]
+    own, own_enc, own_bias, *own_next = load(
+        [acts[0], enc_weight, enc_bias] + ([dec_weight] if ahead else []), ahead, layers
+    )
+    own_dec = load([dec_weight], [0], layers)[0]
+    dec_next = (own_next or [own_dec]) + dec
     enc, dec, bias = [own_enc] + enc, [own_dec] + dec, [own_bias] + bias
     block = own.shape[0]
     rows = block * outer
@@ -181,14 +199,13 @@
         return [jax.ShapeDtypeStruct((size, width), dtype) for size in sizes]
 
     totals = [[] for _ in groups]
-    later = list(range(layers - 1, 0, -1))
     for k, (x, where) in enumerate(xs):
-        plan = [(d, len(groups) if k else 1) for d in later] + ([] if k else [(0, len(groups))])
+        plan = [(d, len(groups) if k else 1) for d in later]
         outs = [shape for d, _ in plan for shape in shapes(BF16 if d else F32, d > 0 and k == 0)]
         latent, *parts = call(
             functools.partial(encode_kernel, core, [where[j] for j in order], plan, layers),
             [hidden] + outs,
-            x + enc + bias + dec,
+            x + enc + bias + dec_next,
             scratch=[pltpu.VMEM((rows, width), BF16)],
             flops=flops * (1 + len(plan)),
         )
@@ -199,8 +216,14 @@
                 for total, group in zip(totals, groups):
                     total.append((at, got))
                     at += block * len(group)
-            for total in totals:
-                total.insert(0, (0, parts.pop(0)))
+            kept = call(
+                functools.partial(decode_kernel, core, layers),
+                shapes(F32),
+                [latent] + dec,
+                flops=flops,
+            )
+            for total, part in zip(totals, kept):
+                total.insert(0, (0, part))
         else:
             own_parts = call(
                 functools.partial(decode_kernel, core, layers),

time: 35.3 us -> 33.2 us (0.941)
  the two profiles are of different devices: /device:TPU:0 before, /device:TPU:3 now
where the time goes in v2:
time: 33.2 us; the launch traced here: 33 us
  starting transfers between devices  16.6 us (50%)
  waiting for transfers between devices  10.1 us (30%)
  Pallas kernels  5.53 us (17%)
  other arithmetic  0.67 us (2%)
    ppermute x11, starting transfers between devices, swap(): return lax.ppermute(x, 'lat', [(i, i ^ k) for i in range(n)])  12.8 us
    pallas_call x10, Pallas kernels, call(): pl.pallas_call(kernel, out_shape=outs, in_specs=specs or [VMEM] * len(arg...  5.53 us
    ppermute x11, waiting for transfers between devices, swap(): return lax.ppermute(x, 'lat', [(i, i ^ k) for i in range(n)])  5.49 us
    ppermute x5, waiting for transfers between devices, send(): return lax.ppermute(part, ('layer', 'lat'), pairs)  4.61 us
    ppermute x5, starting transfers between devices, send(): return lax.ppermute(part, ('layer', 'lat'), pairs)  3.87 us
  transfers between devices with their start and end apart: 16, of which 7 were waited for; matrix products, arithmetic and copies ran while one was open for 0% of the time, Pallas kernels for 17%

profile of v2, /device:TPU:3, one launch (start us, length us, event | category | flops | bytes accessed | tf_op | source)
XLA Modules:
  0.0 33.0 jit_solution(10247327513274370910)
XLA Ops:
  0.0 0.7 %collective-permute-start.5 = (bf16[1,2,512,1280]{3,2,1,0:T(8,128)(2,1)}, bf16[1,2,512,1280]{3,2,1,0:T(8,128)(2,1)S(1)}, u32[]{:S(2)}, u32[]{:S(2)}) collective-permute-start(bf16[1,2,512,1280]{3,2,1,0:T(8,128)(2,1)} %refs_0_.1), channel_id=1, source_target_pairs={{0,1},{1,0},{2,3},{3,2},{4,5},{5,4},{6,7},{7,6},{8,9},{9,8},{10,11... | collective-permute-start | bytes 7864328 | tf_op jit(solution)/shard_map/ppermute | solution.py:29
  0.7 0.0 collective-permute-start.3
  0.7 0.0 copy-start.1
  0.7 2.7 %collective-permute-start.1 = (bf16[16,1280]{1,0:T(8,128)(2,1)}, bf16[16,1280]{1,0:T(8,128)(2,1)S(1)}, u32[]{:S(2)}, u32[]{:S(2)}) collective-permute-start(bf16[16,1280]{1,0:T(8,128)(2,1)} %bitcast.3), channel_id=1, source_target_pairs={{0,9},{1,8},{2,11},{3,10},{4,13},{5,12},{6,15},{7,14},{8,1},{9,0},... | collective-permute-start | bytes 122888 | tf_op jit(solution)/shard_map/ppermute | solution.py:29
  3.4 1.2 %collective-permute-start = (bf16[16,1280]{1,0:T(8,128)(2,1)}, bf16[16,1280]{1,0:T(8,128)(2,1)S(1)}, u32[]{:S(2)}, u32[]{:S(2)}) collective-permute-start(bf16[16,1280]{1,0:T(8,128)(2,1)} %bitcast.4), channel_id=1, source_target_pairs={{0,5},{1,4},{2,7},{3,6},{4,1},{5,0},{6,3},{7,2},{8,13},{9,12},{10,... | collective-permute-start | bytes 122888 | tf_op jit(solution)/shard_map/ppermute | solution.py:29
  4.6 0.3 %collective-permute-start.2 = (bf16[16,1280]{1,0:T(8,128)(2,1)}, bf16[16,1280]{1,0:T(8,128)(2,1)S(1)}, u32[]{:S(2)}, u32[]{:S(2)}) collective-permute-start(bf16[16,1280]{1,0:T(8,128)(2,1)} %bitcast.5), channel_id=1, source_target_pairs={{0,13},{1,12},{2,15},{3,14},{4,9},{5,8},{6,11},{7,10},{8,5},{9,4},... | collective-permute-start | bytes 122888 | tf_op jit(solution)/shard_map/ppermute | solution.py:29
  4.9 1.8 %shard_map.55 = (bf16[16,1280]{1,0:T(8,128)(2,1)S(1)}, bf16[1,1280,512]{2,1,0:T(8,128)(2,1)S(1)}, f32[1,512]{1,0:T(1,128)S(1)}, bf16[1,1,512,1280]{3,2,1,0:T(8,128)(2,1)S(1)}) custom-call(bf16[16,1280]{1,0:T(8,128)(2,1)} %bitcast.6, bf16[1,1280,512]{2,1,0:T(8,128)(2,1)} %refs_1_.1, f32[1,512]{1,0:T(1,128)} %refs_2_.1, bf16[1,2,512,1280]{3,2,1,0:T(8,128)(2,1)} %refs_0_.1), custom_call_target="tpu_custom_call" | custom-call | flops 1000000 | bytes 1048576 | tf_op jit(solution)/shard_map/pallas_call | solution.py:33
  6.7 0.0 collective-permute-done.1.refs_2_.refs_1_
  6.7 0.3 collective-permute-done.refs_1_.refs_0_
  7.0 1.2 %collective-permute-start.8 = (bf16[32,1280]{1,0:T(8,128)(2,1)S(1)}, bf16[32,1280]{1,0:T(8,128)(2,1)S(1)}, u32[]{:S(2)}, u32[]{:S(2)}) collective-permute-start(bf16[32,1280]{1,0:T(8,128)(2,1)S(1)} %shard_map.60), channel_id=1, source_target_pairs={{0,2},{1,3},{2,0},{3,1},{4,6},{5,7},{6,4},{7,5},{8,10},{9,11},{10,... | collective-permute-start | bytes 245768 | tf_op jit(solution)/shard_map/ppermute | solution.py:29
  8.3 2.1 %collective-permute-done.2.refs_3_.refs_1_ = bf16[16,1280]{1,0:T(8,128)(2,1)S(1)} collective-permute-done((bf16[16,1280]{1,0:T(8,128)(2,1)}, bf16[16,1280]{1,0:T(8,128)(2,1)S(1)}, u32[]{:S(2)}, u32[]{:S(2)}) %collective-permute-start.2) | collective-permute-done | bytes 40992 | tf_op jit(solution)/shard_map/ppermute | solution.py:29
  10.4 1.2 %collective-permute-start.7 = (bf16[32,1280]{1,0:T(8,128)(2,1)S(1)}, bf16[32,1280]{1,0:T(8,128)(2,1)S(1)}, u32[]{:S(2)}, u32[]{:S(2)}) collective-permute-start(bf16[32,1280]{1,0:T(8,128)(2,1)S(1)} %shard_map.59), channel_id=1, source_target_pairs={{0,2},{1,3},{2,0},{3,1},{4,6},{5,7},{6,4},{7,5},{8,10},{9,11},{10,... | collective-permute-start | bytes 245768 | tf_op jit(solution)/shard_map/ppermute | solution.py:29
  11.6 0.0 copy-done.1
  11.6 0.7 %collective-permute-start.4 = (f32[1,512]{1,0:T(1,128)S(1)}, f32[1,512]{1,0:T(1,128)S(1)}, u32[]{:S(2)}, u32[]{:S(2)}) collective-permute-start(f32[1,512]{1,0:T(1,128)S(1)} %copy-done.1), channel_id=1, source_target_pairs={{0,1},{1,0},{2,3},{3,2},{4,5},{5,4},{6,7},{7,6},{8,9},{9,8},{10,11... | collective-permute-start | bytes 6152 | tf_op jit(solution)/shard_map/ppermute | solution.py:29
  12.3 0.8 %collective-permute-done.4.refs_7_.refs_5_ = f32[1,512]{1,0:T(1,128)S(1)} collective-permute-done((f32[1,512]{1,0:T(1,128)S(1)}, f32[1,512]{1,0:T(1,128)S(1)}, u32[]{:S(2)}, u32[]{:S(2)}) %collective-permute-start.4) | collective-permute-done | bytes 2080 | tf_op jit(solution)/shard_map/ppermute | solution.py:29
  13.1 0.0 collective-permute-done.3.refs_5_.refs_3_
  13.1 0.0 collective-permute-done.5.refs_9_.refs_1_.refs_7_
  13.1 0.6 %shard_map.56 = (bf16[64,1024]{1,0:T(8,128)(2,1)S(1)}, bf16[64,1280]{1,0:T(8,128)(2,1)S(1)}) custom-call(bf16[16,1280]{1,0:T(8,128)(2,1)S(1)} %get-tuple-element.22.refs_0_, bf16[16,1280]{1,0:T(8,128)(2,1)S(1)} %collective-permute-done.refs_1_.refs_0_, bf16[16,1280]{1,0:T(8,128)(2,1)S(1)} %collective-permute-done.1.refs_2_.refs_1_, ...), custom_call_target="tpu_custom_call" | custom-call | flops 335544320 | bytes 1048576 | tf_op jit(solution)/shard_map/pallas_call | solution.py:33
  13.7 0.9 %collective-permute-start.6 = (bf16[64,1280]{1,0:T(8,128)(2,1)S(1)}, bf16[64,1280]{1,0:T(8,128)(2,1)S(1)}, u32[]{:S(2)}, u32[]{:S(2)}) collective-permute-start(bf16[64,1280]{1,0:T(8,128)(2,1)S(1)} %get-tuple-element.28), channel_id=1, source_target_pairs={{0,16},{1,17},{2,18},{3,19},{4,20},{5,21},{6,22},{7,23},{8,24},{9,... | collective-permute-start | bytes 491528 | tf_op jit(solution)/shard_map/ppermute | solution.py:195
  14.6 1.3 %shard_map.57.refs_0_ = bf16[1,1,512,1280]{3,2,1,0:T(8,128)(2,1)S(1)} custom-call(bf16[1,2,512,1280]{3,2,1,0:T(8,128)(2,1)} %refs_0_.1), custom_call_target="tpu_custom_call" | custom-call | flops 1000000 | bytes 1048576 | tf_op jit(solution)/shard_map/pallas_call | solution.py:33
  15.9 0.0 collective-permute-done.8.refs_1_
  15.9 0.0 collective-permute-done.7.refs_0_
  16.0 0.6 %shard_map.61 = (bf16[64,1024]{1,0:T(8,128)(2,1)S(1)}, bf16[32,1280]{1,0:T(8,128)(2,1)S(1)}, bf16[32,1280]{1,0:T(8,128)(2,1)S(1)}) custom-call(bf16[32,1280]{1,0:T(8,128)(2,1)S(1)} %collective-permute-done.7.refs_0_, bf16[32,1280]{1,0:T(8,128)(2,1)S(1)} %collective-permute-done.8.refs_1_, bf16[1,1280,512]{2,1,0:T(8,128)(2,1)S(1)} %get-tuple-element.23.refs_4_.refs_2_, ...), custom_call_target="tpu_custom_call" | custom-call | flops 335544320 | bytes 1048576 | tf_op jit(solution)/shard_map/pallas_call | solution.py:33
  16.5 1.3 %collective-permute-start.11 = (bf16[32,1280]{1,0:T(8,128)(2,1)S(1)}, bf16[32,1280]{1,0:T(8,128)(2,1)S(1)}, u32[]{:S(2)}, u32[]{:S(2)}) collective-permute-start(bf16[32,1280]{1,0:T(8,128)(2,1)S(1)} %get-tuple-element.34), channel_id=1, source_target_pairs={{0,18},{1,19},{2,16},{3,17},{4,22},{5,23},{6,20},{7,21},{8,26},{9,... | collective-permute-start | bytes 245768 | tf_op jit(solution)/shard_map/ppermute | solution.py:195
  17.8 0.6 %shard_map.62 = (bf16[32,1280]{1,0:T(8,128)(2,1)S(1)}, bf16[32,1280]{1,0:T(8,128)(2,1)S(1)}) custom-call(bf16[64,1024]{1,0:T(8,128)(2,1)S(1)} %get-tuple-element.30.latent, bf16[1,1,512,1280]{3,2,1,0:T(8,128)(2,1)S(1)} %shard_map.57.refs_0_, bf16[1,2,512,1280]{3,2,1,0:T(8,128)(2,1)S(1)} %collective-permute-done.5.refs_9_.refs_1_.refs_7_), custom_call_target="tpu_custom_call" | custom-call | flops 167772160 | bytes 1048576 | tf_op jit(solution)/shard_map/pallas_call | solution.py:33
  18.4 0.3 collective-permute-start.12
  18.7 1.2 %collective-permute-start.9 = (bf16[32,1280]{1,0:T(8,128)(2,1)S(1)}, bf16[32,1280]{1,0:T(8,128)(2,1)S(1)}, u32[]{:S(2)}, u32[]{:S(2)}) collective-permute-start(bf16[32,1280]{1,0:T(8,128)(2,1)S(1)} %get-tuple-element.29), channel_id=1, source_target_pairs={{0,18},{1,19},{2,16},{3,17},{4,22},{5,23},{6,20},{7,21},{8,26},{9,... | collective-permute-start | bytes 245768 | tf_op jit(solution)/shard_map/ppermute | solution.py:195
  19.9 0.2 collective-permute-start.10
  20.1 0.0 copy-start
  20.1 0.6 %shard_map.58 = (f32[32,1280]{1,0:T(8,128)S(1)}, f32[32,1280]{1,0:T(8,128)S(1)}) custom-call(bf16[64,1024]{1,0:T(8,128)(2,1)S(1)} %get-tuple-element.26.latent, bf16[1,1,512,1280]{3,2,1,0:T(8,128)(2,1)S(1)} %shard_map.57.refs_0_, bf16[1,2,512,1280]{3,2,1,0:T(8,128)(2,1)S(1)} %collective-permute-done.5.refs_9_.refs_1_.refs_7_), custom_call_target="tpu_custom_call" | custom-call | flops 167772160 | bytes 1048576 | tf_op jit(solution)/shard_map/pallas_call | solution.py:33
  20.7 0.1 collective-permute-done.11.refs_2_
  20.8 4.5 %collective-permute-done.12.refs_3_ = bf16[32,1280]{1,0:T(8,128)(2,1)S(1)} collective-permute-done((bf16[32,1280]{1,0:T(8,128)(2,1)S(1)}, bf16[32,1280]{1,0:T(8,128)(2,1)S(1)}, u32[]{:S(2)}, u32[]{:S(2)}) %collective-permute-start.12) | collective-permute-done | bytes 81952 | tf_op jit(solution)/shard_map/ppermute | solution.py:195
  25.3 0.0 collective-permute-done.6.refs_1_
  25.3 1.9 %collective-permute-start.13 = (bf16[16,1280]{1,0:T(8,128)(2,1)S(1)}, bf16[16,1280]{1,0:T(8,128)(2,1)S(1)}, u32[]{:S(2)}, u32[]{:S(2)}) collective-permute-start(bf16[16,1280]{1,0:T(8,128)(2,1)S(1)} %get-tuple-element.36), channel_id=1, source_target_pairs={{0,13},{1,12},{2,15},{3,14},{4,9},{5,8},{6,11},{7,10},{8,5},{9,4},... | collective-permute-start | bytes 122888 | tf_op jit(solution)/shard_map/ppermute | solution.py:29
  27.2 0.0 collective-permute-start.14
  27.2 0.0 collective-permute-done.9.refs_2_
  27.2 0.0 collective-permute-done.10.refs_3_
  27.3 2.9 %collective-permute-start.15 = (bf16[16,1280]{1,0:T(8,128)(2,1)S(1)}, bf16[16,1280]{1,0:T(8,128)(2,1)S(1)}, u32[]{:S(2)}, u32[]{:S(2)}) collective-permute-start(bf16[16,1280]{1,0:T(8,128)(2,1)S(1)} %get-tuple-element.38), channel_id=1, source_target_pairs={{0,5},{1,4},{2,7},{3,6},{4,1},{5,0},{6,3},{7,2},{8,13},{9,12},{10,... | collective-permute-start | bytes 122888 | tf_op jit(solution)/shard_map/ppermute | solution.py:29
  30.1 0.0 copy-done
  30.1 1.0 %collective-permute-done.13 = bf16[16,1280]{1,0:T(8,128)(2,1)S(1)} collective-permute-done((bf16[16,1280]{1,0:T(8,128)(2,1)S(1)}, bf16[16,1280]{1,0:T(8,128)(2,1)S(1)}, u32[]{:S(2)}, u32[]{:S(2)}) %collective-permute-start.13) | collective-permute-done | bytes 40992 | tf_op jit(solution)/shard_map/ppermute | solution.py:29
  31.2 1.2 %collective-permute-done.14 = bf16[16,1280]{1,0:T(8,128)(2,1)S(1)} collective-permute-done((bf16[16,1280]{1,0:T(8,128)(2,1)S(1)}, bf16[16,1280]{1,0:T(8,128)(2,1)S(1)}, u32[]{:S(2)}, u32[]{:S(2)}) %collective-permute-start.14) | collective-permute-done | bytes 40992 | tf_op jit(solution)/shard_map/ppermute | solution.py:29
  32.4 0.0 collective-permute-done.15
  32.4 0.6 %fusion = bf16[1,16,1280]{2,1,0:T(8,128)(2,1)} fusion(bf16[16,1280]{1,0:T(8,128)(2,1)S(1)} %collective-permute-done.15, bf16[16,1280]{1,0:T(8,128)(2,1)S(1)} %collective-permute-done.14, f32[16,1280]{1,0:T(8,128)S(1)} %get-tuple-element.32, bf16[16,1280]{1,0:T(8,128)(2,1)S(1)} %collective-permute-done.13, f32[1280]{0:T(1024)S(1)} %reduce), kind=kLoop, calls=%fused_computation.1 | loop fusion | flops 163840 | bytes 250880 | tf_op jit(solution)/shard_map/broadcast_in_dim | solution.py:253
  (5 shorter events, 0.1 us)
Async XLA Ops:
  0.0 13.1 %collective-permute-start.5 = (bf16[1,2,512,1280]{3,2,1,0:T(8,128)(2,1)}, bf16[1,2,512,1280]{3,2,1,0:T(8,128)(2,1)S(1)}, u32[]{:S(2)}, u32[]{:S(2)}) collective-permute-start(bf16[1,2,512,1280]{3,2,1,0:T(8,128)(2,1)} %refs_0_.1), channel_id=1, source_target_pairs={{0,1},{1,0},{2,3},{3,2},{4,5},{5,4},{6,7},{7,6},{8,9},{9,8},{10,11... | collective-permute-start | bytes 7864328 | tf_op jit(solution)/shard_map/ppermute | solution.py:29
  0.7 12.4 %collective-permute-start.3 = (bf16[1,1280,512]{2,1,0:T(8,128)(2,1)}, bf16[1,1280,512]{2,1,0:T(8,128)(2,1)S(1)}, u32[]{:S(2)}, u32[]{:S(2)}) collective-permute-start(bf16[1,1280,512]{2,1,0:T(8,128)(2,1)} %refs_1_.1), channel_id=1, source_target_pairs={{0,1},{1,0},{2,3},{3,2},{4,5},{5,4},{6,7},{7,6},{8,9},{9,8},{10,11... | collective-permute-start | bytes 3932168 | tf_op jit(solution)/shard_map/ppermute | solution.py:29
  0.7 10.9 %copy-start.1 = (f32[1,512]{1,0:T(1,128)S(1)}, f32[1,512]{1,0:T(1,128)}, u32[]{:S(2)}) copy-start(f32[1,512]{1,0:T(1,128)} %refs_2_.1) | copy-start | bytes 6148
  0.7 6.0 %collective-permute-start.1 = (bf16[16,1280]{1,0:T(8,128)(2,1)}, bf16[16,1280]{1,0:T(8,128)(2,1)S(1)}, u32[]{:S(2)}, u32[]{:S(2)}) collective-permute-start(bf16[16,1280]{1,0:T(8,128)(2,1)} %bitcast.3), channel_id=1, source_target_pairs={{0,9},{1,8},{2,11},{3,10},{4,13},{5,12},{6,15},{7,14},{8,1},{9,0},... | collective-permute-start | bytes 122888 | tf_op jit(solution)/shard_map/ppermute | solution.py:29
  3.4 3.6 %collective-permute-start = (bf16[16,1280]{1,0:T(8,128)(2,1)}, bf16[16,1280]{1,0:T(8,128)(2,1)S(1)}, u32[]{:S(2)}, u32[]{:S(2)}) collective-permute-start(bf16[16,1280]{1,0:T(8,128)(2,1)} %bitcast.4), channel_id=1, source_target_pairs={{0,5},{1,4},{2,7},{3,6},{4,1},{5,0},{6,3},{7,2},{8,13},{9,12},{10,... | collective-permute-start | bytes 122888 | tf_op jit(solution)/shard_map/ppermute | solution.py:29
  4.6 5.8 %collective-permute-start.2 = (bf16[16,1280]{1,0:T(8,128)(2,1)}, bf16[16,1280]{1,0:T(8,128)(2,1)S(1)}, u32[]{:S(2)}, u32[]{:S(2)}) collective-permute-start(bf16[16,1280]{1,0:T(8,128)(2,1)} %bitcast.5), channel_id=1, source_target_pairs={{0,13},{1,12},{2,15},{3,14},{4,9},{5,8},{6,11},{7,10},{8,5},{9,4},... | collective-permute-start | bytes 122888 | tf_op jit(solution)/shard_map/ppermute | solution.py:29
  7.0 8.9 %collective-permute-start.8 = (bf16[32,1280]{1,0:T(8,128)(2,1)S(1)}, bf16[32,1280]{1,0:T(8,128)(2,1)S(1)}, u32[]{:S(2)}, u32[]{:S(2)}) collective-permute-start(bf16[32,1280]{1,0:T(8,128)(2,1)S(1)} %shard_map.60), channel_id=1, source_target_pairs={{0,2},{1,3},{2,0},{3,1},{4,6},{5,7},{6,4},{7,5},{8,10},{9,11},{10,... | collective-permute-start | bytes 245768 | tf_op jit(solution)/shard_map/ppermute | solution.py:29
  10.4 5.6 %collective-permute-start.7 = (bf16[32,1280]{1,0:T(8,128)(2,1)S(1)}, bf16[32,1280]{1,0:T(8,128)(2,1)S(1)}, u32[]{:S(2)}, u32[]{:S(2)}) collective-permute-start(bf16[32,1280]{1,0:T(8,128)(2,1)S(1)} %shard_map.59), channel_id=1, source_target_pairs={{0,2},{1,3},{2,0},{3,1},{4,6},{5,7},{6,4},{7,5},{8,10},{9,11},{10,... | collective-permute-start | bytes 245768 | tf_op jit(solution)/shard_map/ppermute | solution.py:29
  11.6 1.5 %collective-permute-start.4 = (f32[1,512]{1,0:T(1,128)S(1)}, f32[1,512]{1,0:T(1,128)S(1)}, u32[]{:S(2)}, u32[]{:S(2)}) collective-permute-start(f32[1,512]{1,0:T(1,128)S(1)} %copy-done.1), channel_id=1, source_target_pairs={{0,1},{1,0},{2,3},{3,2},{4,5},{5,4},{6,7},{7,6},{8,9},{9,8},{10,11... | collective-permute-start | bytes 6152 | tf_op jit(solution)/shard_map/ppermute | solution.py:29
  13.7 11.6 %collective-permute-start.6 = (bf16[64,1280]{1,0:T(8,128)(2,1)S(1)}, bf16[64,1280]{1,0:T(8,128)(2,1)S(1)}, u32[]{:S(2)}, u32[]{:S(2)}) collective-permute-start(bf16[64,1280]{1,0:T(8,128)(2,1)S(1)} %get-tuple-element.28), channel_id=1, source_target_pairs={{0,16},{1,17},{2,18},{3,19},{4,20},{5,21},{6,22},{7,23},{8,24},{9,... | collective-permute-start | bytes 491528 | tf_op jit(solution)/shard_map/ppermute | solution.py:195
  16.5 4.2 %collective-permute-start.11 = (bf16[32,1280]{1,0:T(8,128)(2,1)S(1)}, bf16[32,1280]{1,0:T(8,128)(2,1)S(1)}, u32[]{:S(2)}, u32[]{:S(2)}) collective-permute-start(bf16[32,1280]{1,0:T(8,128)(2,1)S(1)} %get-tuple-element.34), channel_id=1, source_target_pairs={{0,18},{1,19},{2,16},{3,17},{4,22},{5,23},{6,20},{7,21},{8,26},{9,... | collective-permute-start | bytes 245768 | tf_op jit(solution)/shard_map/ppermute | solution.py:195
  18.4 6.9 %collective-permute-start.12 = (bf16[32,1280]{1,0:T(8,128)(2,1)S(1)}, bf16[32,1280]{1,0:T(8,128)(2,1)S(1)}, u32[]{:S(2)}, u32[]{:S(2)}) collective-permute-start(bf16[32,1280]{1,0:T(8,128)(2,1)S(1)} %get-tuple-element.35), channel_id=1, source_target_pairs={{0,2},{1,3},{2,0},{3,1},{4,6},{5,7},{6,4},{7,5},{8,10},{9,11},{10,... | collective-permute-start | bytes 245768 | tf_op jit(solution)/shard_map/ppermute | solution.py:195
  18.7 8.5 %collective-permute-start.9 = (bf16[32,1280]{1,0:T(8,128)(2,1)S(1)}, bf16[32,1280]{1,0:T(8,128)(2,1)S(1)}, u32[]{:S(2)}, u32[]{:S(2)}) collective-permute-start(bf16[32,1280]{1,0:T(8,128)(2,1)S(1)} %get-tuple-element.29), channel_id=1, source_target_pairs={{0,18},{1,19},{2,16},{3,17},{4,22},{5,23},{6,20},{7,21},{8,26},{9,... | collective-permute-start | bytes 245768 | tf_op jit(solution)/shard_map/ppermute | solution.py:195
  19.9 7.3 %collective-permute-start.10 = (bf16[32,1280]{1,0:T(8,128)(2,1)S(1)}, bf16[32,1280]{1,0:T(8,128)(2,1)S(1)}, u32[]{:S(2)}, u32[]{:S(2)}) collective-permute-start(bf16[32,1280]{1,0:T(8,128)(2,1)S(1)} %get-tuple-element.31), channel_id=1, source_target_pairs={{0,2},{1,3},{2,0},{3,1},{4,6},{5,7},{6,4},{7,5},{8,10},{9,11},{10,... | collective-permute-start | bytes 245768 | tf_op jit(solution)/shard_map/ppermute | solution.py:195
  20.1 10.0 %copy-start = (f32[1,1280]{1,0:T(1,128)S(1)}, f32[1,1280]{1,0:T(1,128)}, u32[]{:S(2)}) copy-start(f32[1,1280]{1,0:T(1,128)} %param.9) | copy-start | bytes 15364
  25.3 5.8 %collective-permute-start.13 = (bf16[16,1280]{1,0:T(8,128)(2,1)S(1)}, bf16[16,1280]{1,0:T(8,128)(2,1)S(1)}, u32[]{:S(2)}, u32[]{:S(2)}) collective-permute-start(bf16[16,1280]{1,0:T(8,128)(2,1)S(1)} %get-tuple-element.36), channel_id=1, source_target_pairs={{0,13},{1,12},{2,15},{3,14},{4,9},{5,8},{6,11},{7,10},{8,5},{9,4},... | collective-permute-start | bytes 122888 | tf_op jit(solution)/shard_map/ppermute | solution.py:29
  27.2 5.2 %collective-permute-start.14 = (bf16[16,1280]{1,0:T(8,128)(2,1)S(1)}, bf16[16,1280]{1,0:T(8,128)(2,1)S(1)}, u32[]{:S(2)}, u32[]{:S(2)}) collective-permute-start(bf16[16,1280]{1,0:T(8,128)(2,1)S(1)} %get-tuple-element.37), channel_id=1, source_target_pairs={{0,9},{1,8},{2,11},{3,10},{4,13},{5,12},{6,15},{7,14},{8,1},{9,0},... | collective-permute-start | bytes 122888 | tf_op jit(solution)/shard_map/ppermute | solution.py:29
  27.3 5.1 %collective-permute-start.15 = (bf16[16,1280]{1,0:T(8,128)(2,1)S(1)}, bf16[16,1280]{1,0:T(8,128)(2,1)S(1)}, u32[]{:S(2)}, u32[]{:S(2)}) collective-permute-start(bf16[16,1280]{1,0:T(8,128)(2,1)S(1)} %get-tuple-element.38), channel_id=1, source_target_pairs={{0,5},{1,4},{2,7},{3,6},{4,1},{5,0},{6,3},{7,2},{8,13},{9,12},{10,... | collective-permute-start | bytes 122888 | tf_op jit(solution)/shard_map/ppermute | solution.py:29
